TPU v7x, 32 devices: a whole 2x2x4 slice. The times are simulated.
32 devices in a mesh: seq: 2 (over y), dp: 16 (over z, x, core).
Axes of the slice: x: 2, y: 2, z: 4, core: 2. Of those that a mesh axis runs over, the one named last changes fastest.
Arguments:
- inputs: bfloat16 [16, 2, 1024, 768], P('dp', None, 'seq'), may hold values from -6 to 6
- query_weight: bfloat16 [768, 768], P(('seq', 'dp')), may hold values from -0.21875 to 0.21875
- key_weight: bfloat16 [768, 768], P(('seq', 'dp')), may hold values from -0.21875 to 0.21875
- value_weight: bfloat16 [768, 768], P(('seq', 'dp')), may hold values from -0.21875 to 0.21875
- query_bias: bfloat16 [768], P(('seq', 'dp')), may hold values from -3 to 3
- value_bias: bfloat16 [768], P(('seq', 'dp')), may hold values from -3 to 3
- output_weight: bfloat16 [768, 768], P(('seq', 'dp')), may hold values from -2.5 to 2.5
- output_bias: bfloat16 [768], P(('seq', 'dp')), may hold values from -3 to 3
- first_gain: bfloat16 [768], P(('seq', 'dp')), may hold values from 0.099609375 to 1.8984375
- first_shift: bfloat16 [768], P(('seq', 'dp')), may hold values from -3 to 3
- inner_weight: bfloat16 [768, 3072], P(('seq', 'dp')), may hold values from -0.21875 to 0.21875
- inner_bias: bfloat16 [3072], P(('seq', 'dp')), may hold values from -3 to 3
- outer_weight: bfloat16 [3072, 768], P(('seq', 'dp')), may hold values from -0.109375 to 0.109375
- outer_bias: bfloat16 [768], P(('seq', 'dp')), may hold values from -3 to 3
- second_gain: bfloat16 [768], P(('seq', 'dp')), may hold values from 0.099609375 to 1.8984375
- second_shift: bfloat16 [768], P(('seq', 'dp')), may hold values from -3 to 3
- prefix: int32 [16, 2], P('dp'), may hold values from 102 to 512, as said below
- cotangent: bfloat16 [16, 2, 1024, 768], P('dp', None, 'seq'), may hold values from -6 to 6
Outputs:
- outputs: bfloat16 [16, 2, 1024, 768], P('dp', None, 'seq')
- input_grad: float32 [16, 2, 1024, 768], P('dp', None, 'seq')
- grad_query_weight: float32 [768, 768], P(('seq', 'dp'))
- grad_key_weight: float32 [768, 768], P(('seq', 'dp'))
- grad_value_weight: float32 [768, 768], P(('seq', 'dp'))
- grad_query_bias: float32 [768], P(('seq', 'dp'))
- grad_value_bias: float32 [768], P(('seq', 'dp'))
- grad_output_weight: float32 [768, 768], P(('seq', 'dp'))
- grad_output_bias: float32 [768], P(('seq', 'dp'))
- grad_first_gain: float32 [768], P(('seq', 'dp'))
- grad_first_shift: float32 [768], P(('seq', 'dp'))
- grad_inner_weight: float32 [768, 3072], P(('seq', 'dp'))
- grad_inner_bias: float32 [3072], P(('seq', 'dp'))
- grad_outer_weight: float32 [3072, 768], P(('seq', 'dp'))
- grad_outer_bias: float32 [768], P(('seq', 'dp'))
- grad_second_gain: float32 [768], P(('seq', 'dp'))
- grad_second_shift: float32 [768], P(('seq', 'dp'))
Inputs may be any that keep to these rules, and one draw needn't show every extreme that they name: `prefix`: the number of leading tokens of each sequence that attend to one another both ways; some sequence has 512 and some 1024 // 10.
All inputs are finite; a program needn't handle non-finite values.
Results may differ from a plain program's by a relative error of at most 0.017.
Values may be sent and summed in bfloat16 or wider, within the bound.
A program may use at most 384 MiB of HBM per device.

v0:
```python
import jax
import jax.numpy as jnp
from jax import lax
from jax.sharding import PartitionSpec as P

HEADS = 12
HEAD_DIM = 64


epsilon = 1e-05


def normalize(hidden, gain_vec, shift_vec):
    center = hidden - jnp.mean(hidden, axis=-1, keepdims=True)
    spread = jnp.mean(center * center, axis=-1, keepdims=True)
    return center * lax.rsqrt(spread + epsilon) * gain_vec + shift_vec


def gelu_exact(values):
    return jax.nn.gelu(values, approximate=False)


def dot_float(left_side, right_side):
    return jnp.dot(left_side, right_side, preferred_element_type=jnp.float32)


def dot_back(left_side, right_side):
    return lax.dot_general(
        left_side, right_side, (((1,), (1,)), ((), ())), preferred_element_type=jnp.float32
    )


def row_product(left_side, right_side):
    return lax.dot_general(
        left_side, right_side, (((0,), (0,)), ((), ())), preferred_element_type=jnp.float32
    )


def column_sums(values):
    return jnp.sum(values.astype(jnp.float32), axis=0)


def project_keys(weights, tokens):
    key_low = dot_float(tokens, weights[1]).astype(jnp.bfloat16)
    value_low = (dot_float(tokens, weights[2]) + weights[4].astype(jnp.float32)).astype(
        jnp.bfloat16
    )
    return (key_low, value_low)


def forward_pass(weights, tokens, key_all, value_all, first_pos, prefix_len):
    (
        query_weight,
        key_weight,
        value_weight,
        query_bias,
        value_bias,
        output_weight,
        output_bias,
        first_gain,
        first_shift,
        inner_weight,
        inner_bias,
        outer_weight,
        outer_bias,
        second_gain,
        second_shift,
    ) = weights
    row_count = tokens.shape[0]
    total_rows = key_all.shape[0]
    queries = (dot_float(tokens, query_weight) + query_bias.astype(jnp.float32)).astype(
        jnp.bfloat16
    )
    head_query = queries.reshape(row_count, HEADS, HEAD_DIM)
    head_key = key_all.reshape(total_rows, HEADS, HEAD_DIM)
    head_value = value_all.reshape(total_rows, HEADS, HEAD_DIM)
    scores = (
        jnp.einsum("qhd,khd->hqk", head_query, head_key, preferred_element_type=jnp.float32) * 0.125
    )
    query_pos = first_pos + jnp.arange(row_count, dtype=jnp.int32)
    key_pos = jnp.arange(total_rows, dtype=jnp.int32)
    allowed = (key_pos[None, :] <= query_pos[:, None]) | (key_pos[None, :] < prefix_len)
    scores = jnp.where(allowed[None], scores, -1e30)
    log_total = jax.nn.logsumexp(scores, axis=-1)
    probs = jnp.exp(scores - log_total[:, :, None])
    probs_low = probs.astype(jnp.bfloat16)
    mixed_heads = jnp.einsum(
        "hqk,khd->qhd", probs_low, head_value, preferred_element_type=jnp.float32
    )
    mixed_low = mixed_heads.reshape(row_count, HEADS * HEAD_DIM).astype(jnp.bfloat16)
    branch = dot_float(mixed_low, output_weight) + output_bias.astype(jnp.float32)
    middle, first_pull = jax.vjp(
        normalize,
        tokens.astype(jnp.float32) + branch,
        first_gain.astype(jnp.float32),
        first_shift.astype(jnp.float32),
    )
    middle_low = middle.astype(jnp.bfloat16)
    inner_act = dot_float(middle_low, inner_weight) + inner_bias.astype(jnp.float32)
    hidden, gelu_pull = jax.vjp(gelu_exact, inner_act)
    hidden_low = hidden.astype(jnp.bfloat16)
    outer_act = dot_float(hidden_low, outer_weight) + outer_bias.astype(jnp.float32)
    result, second_pull = jax.vjp(
        normalize,
        middle + outer_act,
        second_gain.astype(jnp.float32),
        second_shift.astype(jnp.float32),
    )
    return (
        head_query,
        head_key,
        head_value,
        probs,
        probs_low,
        mixed_low,
        first_pull,
        middle_low,
        gelu_pull,
        hidden_low,
        second_pull,
        result,
        queries,
        log_total,
    )


def on_device(
    inputs,
    query_weight,
    key_weight,
    value_weight,
    query_bias,
    value_bias,
    output_weight,
    output_bias,
    first_gain,
    first_shift,
    inner_weight,
    inner_bias,
    outer_weight,
    outer_bias,
    second_gain,
    second_shift,
    prefix,
    cotangent,
):
    micro_count = inputs.shape[1]
    row_count = inputs.shape[2]
    first_pos = lax.axis_index("seq") * row_count
    results = []
    kept_pairs = []
    own_pairs = []
    for micro_step in range(micro_count):
        weights = (
            lax.all_gather(query_weight, ("seq", "dp"), axis=0, tiled=True),
            lax.all_gather(key_weight, ("seq", "dp"), axis=0, tiled=True),
            lax.all_gather(value_weight, ("seq", "dp"), axis=0, tiled=True),
            lax.all_gather(query_bias, ("seq", "dp"), axis=0, tiled=True),
            lax.all_gather(value_bias, ("seq", "dp"), axis=0, tiled=True),
            lax.all_gather(output_weight, ("seq", "dp"), axis=0, tiled=True),
            lax.all_gather(output_bias, ("seq", "dp"), axis=0, tiled=True),
            lax.all_gather(first_gain, ("seq", "dp"), axis=0, tiled=True),
            lax.all_gather(first_shift, ("seq", "dp"), axis=0, tiled=True),
            lax.all_gather(inner_weight, ("seq", "dp"), axis=0, tiled=True),
            lax.all_gather(inner_bias, ("seq", "dp"), axis=0, tiled=True),
            lax.all_gather(outer_weight, ("seq", "dp"), axis=0, tiled=True),
            lax.all_gather(outer_bias, ("seq", "dp"), axis=0, tiled=True),
            lax.all_gather(second_gain, ("seq", "dp"), axis=0, tiled=True),
            lax.all_gather(second_shift, ("seq", "dp"), axis=0, tiled=True),
        )
        tokens = inputs[0, micro_step]
        key_low, value_low = project_keys(weights, tokens)
        own_pairs.append((key_low, value_low))
        key_all, value_all = (
            lax.all_gather(key_low, "seq", axis=0, tiled=True),
            lax.all_gather(value_low, "seq", axis=0, tiled=True),
        )
        kept_pairs.append((key_all, value_all))
        stored = forward_pass(weights, tokens, key_all, value_all, first_pos, prefix[0, micro_step])
        results.append(stored[11].astype(jnp.bfloat16))
    totals = None
    input_grads = []
    for micro_step in range(micro_count):
        weights = (
            lax.all_gather(query_weight, ("seq", "dp"), axis=0, tiled=True),
            lax.all_gather(key_weight, ("seq", "dp"), axis=0, tiled=True),
            lax.all_gather(value_weight, ("seq", "dp"), axis=0, tiled=True),
            lax.all_gather(query_bias, ("seq", "dp"), axis=0, tiled=True),
            lax.all_gather(value_bias, ("seq", "dp"), axis=0, tiled=True),
            lax.all_gather(output_weight, ("seq", "dp"), axis=0, tiled=True),
            lax.all_gather(output_bias, ("seq", "dp"), axis=0, tiled=True),
            lax.all_gather(first_gain, ("seq", "dp"), axis=0, tiled=True),
            lax.all_gather(first_shift, ("seq", "dp"), axis=0, tiled=True),
            lax.all_gather(inner_weight, ("seq", "dp"), axis=0, tiled=True),
            lax.all_gather(inner_bias, ("seq", "dp"), axis=0, tiled=True),
            lax.all_gather(outer_weight, ("seq", "dp"), axis=0, tiled=True),
            lax.all_gather(outer_bias, ("seq", "dp"), axis=0, tiled=True),
            lax.all_gather(second_gain, ("seq", "dp"), axis=0, tiled=True),
            lax.all_gather(second_shift, ("seq", "dp"), axis=0, tiled=True),
        )
        (
            full_query,
            full_key,
            full_value,
            full_qbias,
            full_vbias,
            full_output,
            full_obias,
            full_fgain,
            full_fshift,
            full_inner,
            full_ibias,
            full_outer,
            full_outbias,
            full_sgain,
            full_sshift,
        ) = weights
        tokens = inputs[0, micro_step]
        prefix_len = prefix[0, micro_step]
        own_key, own_value = project_keys(weights, tokens)
        key_all, value_all = (
            lax.all_gather(own_key, "seq", axis=0, tiled=True),
            lax.all_gather(own_value, "seq", axis=0, tiled=True),
        )
        (
            head_query,
            head_key,
            head_value,
            probs,
            probs_low,
            mixed_low,
            first_pull,
            middle_low,
            gelu_pull,
            hidden_low,
            second_pull,
            result,
            queries,
            log_total,
        ) = forward_pass(weights, tokens, key_all, value_all, first_pos, prefix_len)
        grad_out = cotangent[0, micro_step].astype(jnp.float32)
        grad_mid2, grad_sgain, grad_sshift = second_pull(grad_out)
        grad_outer = grad_mid2.astype(jnp.bfloat16)
        grad_hidden = dot_back(grad_outer, full_outer).astype(jnp.bfloat16)
        grad_inner = gelu_pull(grad_hidden.astype(jnp.float32))[0].astype(jnp.bfloat16)
        grad_middle = grad_mid2 + dot_back(grad_inner, full_inner)
        grad_sum1, grad_fgain, grad_fshift = first_pull(grad_middle)
        grad_branch = grad_sum1.astype(jnp.bfloat16)
        grad_mixed = dot_back(grad_branch, full_output).astype(jnp.bfloat16)
        head_grad = grad_mixed.reshape(row_count, HEADS, HEAD_DIM)
        grad_probs = jnp.einsum(
            "qhd,khd->hqk", head_grad, head_value, preferred_element_type=jnp.float32
        )
        row_dot = jnp.sum(grad_probs * probs, axis=-1)
        grad_scores = (probs * (grad_probs - row_dot[:, :, None])).astype(jnp.bfloat16)
        grad_queries = (
            (
                jnp.einsum(
                    "hqk,khd->qhd", grad_scores, head_key, preferred_element_type=jnp.float32
                )
                * 0.125
            )
            .reshape(row_count, HEADS * HEAD_DIM)
            .astype(jnp.bfloat16)
        )
        total_rows = head_key.shape[0]
        key_terms = (
            jnp.einsum("hqk,qhd->khd", grad_scores, head_query, preferred_element_type=jnp.float32)
            * 0.125
        ).reshape(total_rows, HEADS * HEAD_DIM)
        value_terms = jnp.einsum(
            "hqk,qhd->khd", probs_low, head_grad, preferred_element_type=jnp.float32
        ).reshape(total_rows, HEADS * HEAD_DIM)
        key_sum, value_sum = (
            lax.psum_scatter(
                key_terms.astype(jnp.bfloat16), "seq", scatter_dimension=0, tiled=True
            ).astype(jnp.float32),
            lax.psum_scatter(
                value_terms.astype(jnp.bfloat16), "seq", scatter_dimension=0, tiled=True
            ).astype(jnp.float32),
        )
        grad_keys = key_sum.astype(jnp.bfloat16)
        grad_values = value_sum.astype(jnp.bfloat16)
        new_terms = (
            row_product(tokens, grad_queries),
            row_product(tokens, grad_keys),
            row_product(tokens, grad_values),
            column_sums(grad_queries),
            column_sums(grad_values),
            row_product(mixed_low, grad_branch),
            column_sums(grad_branch),
            grad_fgain,
            grad_fshift,
            row_product(middle_low, grad_inner),
            column_sums(grad_inner),
            row_product(hidden_low, grad_outer),
            column_sums(grad_outer),
            grad_sgain,
            grad_sshift,
        )
        totals = new_terms if totals is None else jax.tree.map(jnp.add, totals, new_terms)
        grad_tokens = (
            grad_sum1
            + dot_back(grad_queries, full_query)
            + dot_back(grad_keys, full_key)
            + dot_back(grad_values, full_value)
        )
        input_grads.append(grad_tokens)
    (
        total_qw,
        total_kw,
        total_vw,
        total_qb,
        total_vb,
        total_ow,
        total_ob,
        total_fg,
        total_fs,
        total_iw,
        total_ib,
        total_uw,
        total_ub,
        total_sg,
        total_ss,
    ) = totals
    owned = (
        lax.psum_scatter(total_qw, ("seq", "dp"), scatter_dimension=0, tiled=True),
        lax.psum_scatter(total_kw, ("seq", "dp"), scatter_dimension=0, tiled=True),
        lax.psum_scatter(total_vw, ("seq", "dp"), scatter_dimension=0, tiled=True),
        lax.psum_scatter(total_qb, ("seq", "dp"), scatter_dimension=0, tiled=True),
        lax.psum_scatter(total_vb, ("seq", "dp"), scatter_dimension=0, tiled=True),
        lax.psum_scatter(total_ow, ("seq", "dp"), scatter_dimension=0, tiled=True),
        lax.psum_scatter(total_ob, ("seq", "dp"), scatter_dimension=0, tiled=True),
        lax.psum_scatter(total_fg, ("seq", "dp"), scatter_dimension=0, tiled=True),
        lax.psum_scatter(total_fs, ("seq", "dp"), scatter_dimension=0, tiled=True),
        lax.psum_scatter(total_iw, ("seq", "dp"), scatter_dimension=0, tiled=True),
        lax.psum_scatter(total_ib, ("seq", "dp"), scatter_dimension=0, tiled=True),
        lax.psum_scatter(total_uw, ("seq", "dp"), scatter_dimension=0, tiled=True),
        lax.psum_scatter(total_ub, ("seq", "dp"), scatter_dimension=0, tiled=True),
        lax.psum_scatter(total_sg, ("seq", "dp"), scatter_dimension=0, tiled=True),
        lax.psum_scatter(total_ss, ("seq", "dp"), scatter_dimension=0, tiled=True),
    )
    outputs = jnp.stack(results)[None]
    input_grad = jnp.stack(input_grads)[None]
    return (outputs, input_grad) + tuple(owned)


def solution(mesh):
    placed = (
        P("dp", None, "seq", None),
        P(("seq", "dp"), None),
        P(("seq", "dp"), None),
        P(("seq", "dp"), None),
        P(("seq", "dp")),
        P(("seq", "dp")),
        P(("seq", "dp"), None),
        P(("seq", "dp")),
        P(("seq", "dp")),
        P(("seq", "dp")),
        P(("seq", "dp"), None),
        P(("seq", "dp")),
        P(("seq", "dp"), None),
        P(("seq", "dp")),
        P(("seq", "dp")),
        P(("seq", "dp")),
        P("dp", None),
        P("dp", None, "seq", None),
    )
    return jax.shard_map(
        on_device,
        mesh=mesh,
        in_specs=placed,
        out_specs=(
            P("dp", None, "seq", None),
            P("dp", None, "seq", None),
            P(("seq", "dp"), None),
            P(("seq", "dp"), None),
            P(("seq", "dp"), None),
            P(("seq", "dp")),
            P(("seq", "dp")),
            P(("seq", "dp"), None),
            P(("seq", "dp")),
            P(("seq", "dp")),
            P(("seq", "dp")),
            P(("seq", "dp"), None),
            P(("seq", "dp")),
            P(("seq", "dp"), None),
            P(("seq", "dp")),
            P(("seq", "dp")),
            P(("seq", "dp")),
        ),
        check_vma=False,
    )
```

profile of v0, /device:TPU:12, one launch (start us, length us, event | category | flops | bytes accessed | tf_op | source)
XLA Modules:
  0.0 1413.1 jit_solution(9643588016793416233)
XLA Ops:
  9.6 55.5 %all-gather.17.cloned.1.call-done = bf16[768,768]{1,0:T(8,128)(2,1)} async-done(((bf16[24,768]{1,0:T(8,128)(2,1)}), bf16[768,768]{1,0:T(8,128)(2,1)}) %all-gather.17.cloned.1.call-update) | async-done | bytes 1179664 | tf_op jit(solution)/shard_map/all_gather | solution.py:156
  70.5 40.4 %all-reduce.19 = (bf16[768]{0:T(1024)(128)(2,1)S(1)}, bf16[768]{0:T(1024)(128)(2,1)S(1)}, bf16[768]{0:T(1024)(128)(2,1)S(1)}, bf16[768]{0:T(1024)(128)(2,1)S(1)}...) all-reduce(bf16[768]{0:T(1024)(128)(2,1)S(1)} %dynamic-update-slice, ...), channel_id=1, replica_groups=mesh['seq'=2,'dp'=16] {'seq','dp'}, use_global_device_ids=true, to_apply=%add | all-reduce | flops 9216 | bytes 36864
  135.2 41.3 %all-gather.15.cloned.1.call-done = bf16[768,768]{1,0:T(8,128)(2,1)} async-done(((bf16[24,768]{1,0:T(8,128)(2,1)}), bf16[768,768]{1,0:T(8,128)(2,1)}) %all-gather.15.cloned.1.call-update) | async-done | bytes 1179664 | tf_op jit(solution)/shard_map/all_gather | solution.py:155
  183.0 21.1 %all-gather.19.cloned.1.call-done = bf16[1024,768]{1,0:T(8,128)(2,1)} async-done(((bf16[512,768]{1,0:T(8,128)(2,1)}), bf16[1024,768]{1,0:T(8,128)(2,1)}) %all-gather.19.cloned.1.call-update) | async-done | bytes 1572880 | tf_op jit(solution)/shard_map/all_gather | solution.py:175
  206.0 13.0 fusion
  219.1 11.8 exponential_reduce_fusion.1
  246.9 42.4 %all-gather.21.cloned.1.call-done = bf16[768,768]{1,0:T(8,128)(2,1)} async-done(((bf16[24,768]{1,0:T(8,128)(2,1)}), bf16[768,768]{1,0:T(8,128)(2,1)}) %all-gather.21.cloned.1.call-update) | async-done | bytes 1179664 | tf_op jit(solution)/shard_map/all_gather | solution.py:160
  292.6 25.0 %all-gather.29.cloned.1.call-done = bf16[1024,768]{1,0:T(8,128)(2,1)} async-done(((bf16[512,768]{1,0:T(8,128)(2,1)}), bf16[1024,768]{1,0:T(8,128)(2,1)}) %all-gather.29.cloned.1.call-update) | async-done | bytes 1572880 | tf_op jit(solution)/shard_map/all_gather | solution.py:175
  319.3 13.0 fusion.1
  332.4 12.2 exponential_reduce_fusion
  363.5 50.7 %all-gather.23.cloned.1.call-done = bf16[768,3072]{1,0:T(8,128)(2,1)} async-done(((bf16[24,3072]{1,0:T(8,128)(2,1)}), bf16[768,3072]{1,0:T(8,128)(2,1)}) %all-gather.23.cloned.1.call-update) | async-done | bytes 4718608 | tf_op jit(solution)/shard_map/all_gather | solution.py:164
  421.7 34.9 %multiply_convert_fusion.3 = (bf16[512,3072]{1,0:T(8,128)(2,1)}, f32[512,3072]{1,0:T(8,128)}, bf16[512,3072]{1,0:T(8,128)(2,1)}, f32[512,3072]{1,0:T(8,128)}, f32[512,3072]{1,0:T(8,128)}) fusion(f32[3072]{0:T(1024)S(1)} %convert_element_type.302, f32[512,3072]{1,0:T(8,128)S(1)} %fusion.92, bf16[768,3072]{1,0:T(8,128)(2,1)S(1)} %copy-done.75, ...), kind=kOutput, calls=%fused_computation.51 | convolution fusion | flops 2625503232 | bytes 37771264 | tf_op jit(solution)/shard_map/dot_general | solution.py:24
  456.7 22.2 %all-gather.25.cloned.1.call-done = bf16[3072,768]{1,0:T(8,128)(2,1)} async-done(((bf16[96,768]{1,0:T(8,128)(2,1)}), bf16[3072,768]{1,0:T(8,128)(2,1)}) %all-gather.25.cloned.1.call-update) | async-done | bytes 4718608 | tf_op jit(solution)/shard_map/all_gather | solution.py:166
  529.5 13.1 convolution_convert_fusion.3
  542.6 18.7 %multiply_reduce_fusion.1 = (f32[12,512]{1,0:T(8,128)S(1)}, f32[12,512,1024]{2,1,0:T(8,128)}) fusion(f32[12,512,1024]{2,1,0:T(8,128)} %get-tuple-element.137, f32[12,512]{1,0:T(8,128)S(1)} %copy-done.49, pred[512,1024]{1,0:T(8,128)(4,1)} %get-tuple-element.132, bf16[512,12,64]{0,2,1:T(8,128)(2,1)} %bitcast.214, bf16[1024,12,64]{0,2,1:T(8,128)(2,1)} %bitcast.206), kind=kOutput, calls=%fused_computation.3 | convolution fusion | flops 836757504 | bytes 53264384 | tf_op jit(solution)/shard_map/qhd,khd->hqk/dot_general | solution.py:251
  566.3 12.8 convolution_convert_fusion.2
  579.1 20.4 %multiply_reduce_fusion = (f32[12,512]{1,0:T(8,128)S(1)}, f32[12,512,1024]{2,1,0:T(8,128)}) fusion(f32[12,512,1024]{2,1,0:T(8,128)} %get-tuple-element.141, f32[12,512]{1,0:T(8,128)S(1)} %copy-done.51, pred[512,1024]{1,0:T(8,128)(4,1)S(1)} %copy-done.16, bf16[512,12,64]{0,2,1:T(8,128)(2,1)S(1)} %bitcast.216, bf16[1024,12,64]{0,2,1:T(8,128)(2,1)} %bitcast.208), kind=kOutput, calls=%fused_computation.1 | convolution fusion | flops 836757504 | bytes 53264384 | tf_op jit(solution)/shard_map/qhd,khd->hqk/dot_general | solution.py:251
  599.6 42.6 %multiply_convert_fusion = (bf16[12,512,1024]{2,1,0:T(8,128)(2,1)}, bf16[12,512,1024]{2,1,0:T(8,128)(2,1)}) fusion(f32[12,512,1024]{2,1,0:T(8,128)} %get-tuple-element.151, f32[12,512,1024]{2,1,0:T(8,128)} %get-tuple-element.141, f32[12,512]{1,0:T(8,128)S(1)} %get-tuple-element.150, f32[12,512]{1,0:T(8,128)S(1)} %copy-done.51, ...), kind=kLoop, calls=%fused_computation | loop fusion | flops 75497472 | bytes 126976000 | tf_op jit(solution)/shard_map/convert_element_type | solution.py:255
  742.3 42.4 %all-reduce.18 = (f32[768]{0:T(1024)S(1)}, f32[768]{0:T(1024)S(1)}, f32[768]{0:T(1024)S(1)}, f32[768]{0:T(1024)S(1)}, f32[768]{0:T(1024)S(1)}, /*index=5*/f32[30...) all-reduce(f32[768]{0:T(1024)S(1)} %add.405, ...), channel_id=9, replica_groups=mesh['seq'=2,'dp'=16] {'seq','dp'}, use_global_device_ids=true, to_apply=%region_31.32.clone | all-reduce | flops 9216 | bytes 73728
  809.8 104.3 %reduce-scatter.31.cloned.1.call-done = f32[24,768]{1,0:T(8,128)} async-done(((f32[768,768]{1,0:T(8,128)}), f32[24,768]{1,0:T(8,128)}) %reduce-scatter.31.cloned.1.call-update) | async-done | bytes 73744
  914.1 104.3 %reduce-scatter.35.cloned.1.call-done = f32[24,768]{1,0:T(8,128)} async-done(((f32[768,768]{1,0:T(8,128)}), f32[24,768]{1,0:T(8,128)}) %reduce-scatter.35.cloned.1.call-update) | async-done | bytes 73744
  1018.5 104.3 %reduce-scatter.33.cloned.1.call-done = f32[24,768]{1,0:T(8,128)} async-done(((f32[768,768]{1,0:T(8,128)}), f32[24,768]{1,0:T(8,128)}) %reduce-scatter.33.cloned.1.call-update) | async-done | bytes 73744
  1122.8 141.5 %reduce-scatter.29.cloned.1.call-done = f32[96,768]{1,0:T(8,128)} async-done(((f32[3072,768]{1,0:T(8,128)}), f32[96,768]{1,0:T(8,128)}) %reduce-scatter.29.cloned.1.call-update) | async-done | bytes 294928 | tf_op jit(solution)/shard_map/reduce_scatter | solution.py:338
  1264.3 141.5 %reduce-scatter.27.cloned.1.call-done = f32[24,3072]{1,0:T(8,128)} async-done(((f32[768,3072]{1,0:T(8,128)}), f32[24,3072]{1,0:T(8,128)}) %reduce-scatter.27.cloned.1.call-update) | async-done | bytes 294928 | tf_op jit(solution)/shard_map/reduce_scatter | solution.py:336
  (382 shorter events, 267.4 us)
Async XLA Ops:
  7.3 63.0 %copy-start.91 = (bf16[96]{0:T(256)(128)(2,1)S(1)}, bf16[96]{0:T(256)(128)(2,1)}, u32[]{:S(2)}) copy-start(bf16[96]{0:T(256)(128)(2,1)} %param.29) | copy-start | bytes 580
  7.3 113.5 %copy-start = (bf16[1,2,512,768]{3,2,1,0:T(8,128)(2,1)S(1)}, bf16[1,2,512,768]{3,2,1,0:T(8,128)(2,1)}, u32[]{:S(2)}) copy-start(bf16[1,2,512,768]{3,2,1,0:T(8,128)(2,1)} %param.18) | copy-start | bytes 4718596
  7.3 57.8 %all-gather.17.cloned.1.call-start = ((), (), s32[]{:S(2)}) async-start(), calls=%async_computation.13 | async-start | bytes 1216512 | tf_op jit(solution)/shard_map/all_gather | solution.py:156
  8.0 112.8 %all-gather.11.cloned.1.call-start = ((), (), s32[]{:S(2)}) async-start(), calls=%async_computation.10 | async-start | bytes 1216512 | tf_op jit(solution)/shard_map/all_gather | solution.py:157
  8.8 167.8 %all-gather.15.cloned.1.call-start = ((), (), s32[]{:S(2)}) async-start(), calls=%async_computation.12 | async-start | bytes 1216512 | tf_op jit(solution)/shard_map/all_gather | solution.py:155
  9.5 194.6 %all-gather.19.cloned.1.call-start = ((), (), s32[]{:S(2)}) async-start(), calls=%async_computation.14 | async-start | bytes 2359296 | tf_op jit(solution)/shard_map/all_gather | solution.py:175
  68.3 164.4 %all-gather.13.cloned.1.call-start = ((), (), s32[]{:S(2)}) async-start(), calls=%async_computation.11 | async-start | bytes 2359296 | tf_op jit(solution)/shard_map/all_gather | solution.py:176
  123.7 165.6 %all-gather.21.cloned.1.call-start = ((), (), s32[]{:S(2)}) async-start(), calls=%async_computation.15 | async-start | bytes 1216512 | tf_op jit(solution)/shard_map/all_gather | solution.py:160
  124.3 193.3 %all-gather.29.cloned.1.call-start = ((), (), s32[]{:S(2)}) async-start(), calls=%async_computation.19 | async-start | bytes 2359296 | tf_op jit(solution)/shard_map/all_gather | solution.py:175
  127.3 219.6 %all-gather.27.cloned.1.call-start = ((), (), s32[]{:S(2)}) async-start(), calls=%async_computation.18 | async-start | bytes 2359296 | tf_op jit(solution)/shard_map/all_gather | solution.py:176
  129.1 285.2 %all-gather.23.cloned.1.call-start = ((), (), s32[]{:S(2)}) async-start(), calls=%async_computation.16 | async-start | bytes 4866048 | tf_op jit(solution)/shard_map/all_gather | solution.py:164
  129.8 349.1 %all-gather.25.cloned.1.call-start = ((), (), s32[]{:S(2)}) async-start(), calls=%async_computation.17 | async-start | bytes 4866048 | tf_op jit(solution)/shard_map/all_gather | solution.py:166
  130.4 558.6 %reduce-scatter.19.cloned.1.call-start = ((), (), s32[]{:S(2)}) async-start(), calls=%async_computation.21 | async-start | bytes 2359296 | tf_op jit(solution)/shard_map/reduce_scatter | solution.py:278
  132.4 353.0 %copy-start.52 = (f32[768]{0:T(1024)}, f32[768]{0:T(1024)S(1)}, u32[]{:S(2)}) copy-start(f32[768]{0:T(1024)S(1)} %convert_element_type.300) | copy-start | bytes 9220
  363.5 157.8 %copy-start.68 = (f32[512]{0:T(512)}, f32[512]{0:T(512)S(1)}, u32[]{:S(2)}) copy-start(f32[512]{0:T(512)S(1)} %fusion.79) | copy-start | bytes 6148
  561.3 131.1 %reduce-scatter.23.cloned.1.call-start = ((), (), s32[]{:S(2)}) async-start(), calls=%async_computation.23 | async-start | bytes 2359296 | tf_op jit(solution)/shard_map/reduce_scatter | solution.py:278
  599.5 100.2 %reduce-scatter.17.cloned.1.call-start = ((), (), s32[]{:S(2)}) async-start(), calls=%async_computation.20 | async-start | bytes 2359296 | tf_op jit(solution)/shard_map/reduce_scatter | solution.py:275
  650.4 53.1 %reduce-scatter.21.cloned.1.call-start = ((), (), s32[]{:S(2)}) async-start(), calls=%async_computation.22 | async-start | bytes 2359296 | tf_op jit(solution)/shard_map/reduce_scatter | solution.py:275
  658.6 151.2 %reduce-scatter.25.cloned.1.call-start = ((), (), s32[]{:S(2)}) async-start(), calls=%async_computation.24 | async-start | bytes 2433024 | tf_op jit(solution)/shard_map/reduce_scatter | solution.py:332
  662.9 251.2 %reduce-scatter.31.cloned.1.call-start = ((), (), s32[]{:S(2)}) async-start(), calls=%async_computation.27 | async-start | bytes 2433024
  688.9 329.5 %reduce-scatter.35.cloned.1.call-start = ((), (), s32[]{:S(2)}) async-start(), calls=%async_computation.29 | async-start | bytes 2433024
  699.6 423.2 %reduce-scatter.33.cloned.1.call-start = ((), (), s32[]{:S(2)}) async-start(), calls=%async_computation.28 | async-start | bytes 2433024
  710.7 553.6 %reduce-scatter.29.cloned.1.call-start = ((), (), s32[]{:S(2)}) async-start(), calls=%async_computation.26 | async-start | bytes 9732096 | tf_op jit(solution)/shard_map/reduce_scatter | solution.py:338
  722.0 683.8 %reduce-scatter.27.cloned.1.call-start = ((), (), s32[]{:S(2)}) async-start(), calls=%async_computation.25 | async-start | bytes 9732096 | tf_op jit(solution)/shard_map/reduce_scatter | solution.py:336
  (93 other events, 1042.8 us)
Sparse Core Ops, SparseCore 0:
  11.0 54.0 all-gather.16
  68.0 52.7 all-gather.10
  123.7 52.8 all-gather.14
  178.0 26.0 all-gather.18
  205.5 27.1 all-gather.12
  235.4 53.8 all-gather.20
  291.5 26.0 all-gather.28
  319.7 27.1 all-gather.26
  349.8 64.4 all-gather.22
  417.0 61.8 all-gather.24
  561.4 23.6 reduce-scatter.18
  599.6 24.0 reduce-scatter.22
  650.5 24.0 reduce-scatter.16
  677.3 26.1 reduce-scatter.20
  709.2 100.5 reduce-scatter.24
  815.5 98.5 reduce-scatter.30
  919.8 98.5 reduce-scatter.34
  1024.2 98.5 reduce-scatter.32
  1129.3 135.0 reduce-scatter.28
  1270.7 135.0 reduce-scatter.26
where the time goes:
time: 1420 us; the launch traced here: 1410 us
  waiting for transfers between devices  884 us (62%)
  matrix products  296 us (21%)
  other arithmetic  85.9 us (6%)
  blocking collectives  82.8 us (6%)
  local copies, waits for them, and re-layouts  46.7 us (3%)
  between operations  16.1 us (1%)
    unnamed x23, waiting for transfers between devices  317 us
    reduce_scatter x1, waiting for transfers between devices, on_device(): lax.psum_scatter(total_uw, ('seq', 'dp'), scatter_dimension=0, tiled=True)  142 us
    reduce_scatter x1, waiting for transfers between devices, on_device(): lax.psum_scatter(total_iw, ('seq', 'dp'), scatter_dimension=0, tiled=True)  141 us
    unnamed x2, blocking collectives  82.8 us
    dot_general x12, matrix products, dot_float(): return jnp.dot(left_side, right_side, preferred_element_type=jnp.float32)  67.7 us
    all_gather x1, waiting for transfers between devices, on_device(): lax.all_gather(key_weight, ('seq', 'dp'), axis=0, tiled=True)  55.5 us
    all_gather x1, waiting for transfers between devices, on_device(): lax.all_gather(inner_weight, ('seq', 'dp'), axis=0, tiled=True)  50.7 us
    all_gather x2, waiting for transfers between devices, on_device(): lax.all_gather(key_low, 'seq', axis=0, tiled=True)  46 us
  transfers between devices with their start and end apart: 20, of which 17 were waited for; matrix products, arithmetic and copies ran while one was open for 24% of the time, Pallas kernels for 0%

commit v1 on v0

v1 whole, which is shorter than its diff:
```python
import jax
import jax.numpy as jnp
from jax import lax
from jax.sharding import PartitionSpec as P

HEADS = 12
HEAD_DIM = 64
EPS = 1e-05
FAR = 1 << 20
BOTH = ("seq", "dp")
F32 = jnp.float32
BF16 = jnp.bfloat16


def dot(a, b):
    return jnp.dot(a, b, preferred_element_type=F32)


def dot_t(a, b):
    return lax.dot_general(a, b, (((1,), (1,)), ((), ())), preferred_element_type=F32)


def t_dot(a, b):
    return lax.dot_general(a, b, (((0,), (0,)), ((), ())), preferred_element_type=F32)


def norm_parts(v):
    center = v - jnp.mean(v, axis=-1, keepdims=True)
    inv = lax.rsqrt(jnp.mean(center * center, axis=-1, keepdims=True) + EPS)
    return center * inv, inv


def norm_grad(grad, unit, inv, gain):
    g = grad * gain
    mean_g = jnp.mean(g, axis=-1, keepdims=True)
    mean_gu = jnp.mean(g * unit, axis=-1, keepdims=True)
    return inv * (g - mean_g - unit * mean_gu)


def heads_of(v):
    return v.reshape(v.shape[0], HEADS, HEAD_DIM)


def attend(q, k, v, key_pos, limit):
    scores = jnp.einsum("qhd,khd->hqk", heads_of(q), heads_of(k), preferred_element_type=F32) * 0.125
    scores = jnp.where((key_pos[None, :] <= limit[:, None])[None], scores, -1e30)
    top = jnp.max(scores, axis=-1, keepdims=True)
    lse = top[..., 0] + jnp.log(jnp.sum(jnp.exp(scores - top), axis=-1))
    probs = jnp.exp(scores - lse[..., None])
    low = probs.astype(BF16)
    mixed = jnp.einsum("hqk,khd->qhd", low, heads_of(v), preferred_element_type=F32)
    return mixed.reshape(q.shape).astype(BF16), (probs, low)


def attend_back(saved, q, k, v, mixed, grad):
    probs, low = saved
    grad_h = heads_of(grad)
    grad_probs = jnp.einsum("qhd,khd->hqk", grad_h, heads_of(v), preferred_element_type=F32)
    row_dot = jnp.sum(grad_probs * probs, axis=-1, keepdims=True)
    grad_scores = (probs * (grad_probs - row_dot)).astype(BF16)
    gq = jnp.einsum("hqk,khd->qhd", grad_scores, heads_of(k), preferred_element_type=F32) * 0.125
    gk = jnp.einsum("hqk,qhd->khd", grad_scores, heads_of(q), preferred_element_type=F32) * 0.125
    gv = jnp.einsum("hqk,qhd->khd", low, grad_h, preferred_element_type=F32)
    return (
        gq.reshape(q.shape).astype(BF16),
        gk.reshape(k.shape).astype(BF16),
        gv.reshape(v.shape).astype(BF16),
    )


def on_device(
    inputs,
    query_weight,
    key_weight,
    value_weight,
    query_bias,
    value_bias,
    output_weight,
    output_bias,
    first_gain,
    first_shift,
    inner_weight,
    inner_bias,
    outer_weight,
    outer_bias,
    second_gain,
    second_shift,
    prefix,
    cotangent,
):
    micros, rows, width = inputs.shape[1:]
    own = query_weight.shape[0]
    hidden_width = inner_weight.shape[1]
    per = hidden_width // width
    seqs = lax.axis_size("seq")
    seq_at = lax.axis_index("seq")
    first_pos = seq_at * rows
    x = inputs[0]
    flat_x = x.reshape(micros * rows, width)
    row_pos = first_pos + jnp.arange(rows, dtype=jnp.int32)

    if seqs == 2:
        before = lax.ppermute(x, "seq", [(0, 1)])
        key_x = jnp.concatenate([x, before], axis=1)
        key_pos = jnp.concatenate(
            [row_pos, jnp.where(seq_at == 1, jnp.arange(rows, dtype=jnp.int32), FAR)]
        )
    else:
        key_x = lax.all_gather(x, "seq", axis=1, tiled=True)
        key_pos = jnp.arange(seqs * rows, dtype=jnp.int32)
    total_rows = key_x.shape[1]
    flat_key_x = key_x.reshape(micros * total_rows, width)

    vectors = (query_bias, value_bias, output_bias, first_gain, first_shift, outer_bias, second_gain, second_shift)
    small = jnp.concatenate(
        [jnp.stack(vectors, axis=1), inner_bias.reshape(own, per)], axis=1
    )
    small_count = small.shape[1]
    small = jnp.pad(small, ((0, 0), (0, 128 - small_count)))
    first_pack = lax.all_gather(
        jnp.concatenate([query_weight, key_weight, value_weight, small], axis=1), BOTH, axis=0, tiled=True
    )
    second_pack = lax.all_gather(
        jnp.concatenate([output_weight, inner_weight], axis=1), BOTH, axis=0, tiled=True
    )
    full_outer = lax.all_gather(outer_weight, BOTH, axis=0, tiled=True)
    full_query = first_pack[:, :width]
    full_kv = first_pack[:, width : 3 * width]
    small_all = first_pack[:, 3 * width : 3 * width + small_count].astype(F32)
    qb, vb, ob, fg, fs, ub, sg, ss = [small_all[:, i] for i in range(8)]
    ib = small_all[:, 8:].reshape(hidden_width)
    full_output = second_pack[:, :width]
    full_inner = second_pack[:, width:]

    queries = (dot(flat_x, full_query) + qb).astype(BF16).reshape(micros, rows, width)
    kv_bias = jnp.concatenate([jnp.zeros_like(vb), vb])
    keys_values = (dot(flat_key_x, full_kv) + kv_bias).astype(BF16).reshape(micros, total_rows, 2 * width)
    keys, values = keys_values[..., :width], keys_values[..., width:]

    mixed_parts, saved = [], []
    for m in range(micros):
        limit = jnp.maximum(row_pos, prefix[0, m] - 1)
        mixed_m, saved_m = attend(queries[m], keys[m], values[m], key_pos, limit)
        mixed_parts.append(mixed_m)
        saved.append(saved_m)
    mixed = jnp.concatenate(mixed_parts, axis=0)

    unit1, inv1 = norm_parts(flat_x.astype(F32) + dot(mixed, full_output) + ob)
    middle = unit1 * fg + fs
    middle_low = middle.astype(BF16)
    inner = dot(middle_low, full_inner) + ib
    half_cdf = 0.5 * (1.0 + lax.erf(inner * (0.5**0.5)))
    hidden = (inner * half_cdf).astype(BF16)
    slope = half_cdf + inner * jnp.exp(-0.5 * inner * inner) * 0.3989422804014327
    unit2, inv2 = norm_parts(middle + dot(hidden, full_outer) + ub)
    result = (unit2 * sg + ss).astype(BF16)

    cot = cotangent[0].reshape(micros * rows, width).astype(F32)
    g_sgain = jnp.sum(cot * unit2, axis=0)
    g_sshift = jnp.sum(cot, axis=0)
    grad_mid2 = norm_grad(cot, unit2, inv2, sg)
    grad_outer = grad_mid2.astype(BF16)
    g_ubias = jnp.sum(grad_outer.astype(F32), axis=0)
    g_outer = t_dot(hidden, grad_outer).astype(BF16)
    own_outer = lax.psum_scatter(g_outer, BOTH, scatter_dimension=0, tiled=True).astype(F32)
    grad_hidden = dot_t(grad_outer, full_outer).astype(BF16)
    grad_inner = (grad_hidden.astype(F32) * slope).astype(BF16)
    g_ibias = jnp.sum(grad_inner.astype(F32), axis=0)
    g_inner = t_dot(middle_low, grad_inner)
    grad_middle = grad_mid2 + dot_t(grad_inner, full_inner)
    g_fgain = jnp.sum(grad_middle * unit1, axis=0)
    g_fshift = jnp.sum(grad_middle, axis=0)
    grad_sum1 = norm_grad(grad_middle, unit1, inv1, fg)
    grad_branch = grad_sum1.astype(BF16)
    g_obias = jnp.sum(grad_branch.astype(F32), axis=0)
    g_output = t_dot(mixed, grad_branch)
    own_second = lax.psum_scatter(
        jnp.concatenate([g_output, g_inner], axis=1).astype(BF16), BOTH, scatter_dimension=0, tiled=True
    ).astype(F32)
    grad_mixed = dot_t(grad_branch, full_output).astype(BF16).reshape(micros, rows, width)

    gq_parts, gk_parts, gv_parts = [], [], []
    for m in range(micros):
        gq, gk, gv = attend_back(
            saved[m], queries[m], keys[m], values[m], mixed_parts[m], grad_mixed[m]
        )
        gq_parts.append(gq)
        gk_parts.append(gk)
        gv_parts.append(gv)
    grad_q = jnp.concatenate(gq_parts, axis=0)
    grad_kv = jnp.concatenate([jnp.stack(gk_parts), jnp.stack(gv_parts)], axis=-1)
    flat_kv = grad_kv.reshape(micros * total_rows, 2 * width)
    g_qbias = jnp.sum(grad_q.astype(F32), axis=0)
    g_vbias = jnp.sum(flat_kv[:, width:].astype(F32), axis=0)
    g_query = t_dot(flat_x, grad_q)
    g_kv = t_dot(flat_key_x, flat_kv)
    g_small = jnp.concatenate(
        [
            jnp.stack([g_qbias, g_vbias, g_obias, g_fgain, g_fshift, g_ubias, g_sgain, g_sshift], axis=1),
            g_ibias.reshape(width, per),
        ],
        axis=1,
    )
    g_small = jnp.pad(g_small, ((0, 0), (0, 128 - small_count)))
    own_first = lax.psum_scatter(
        jnp.concatenate([g_query, g_kv, g_small], axis=1).astype(BF16), BOTH, scatter_dimension=0, tiled=True
    ).astype(F32)

    via_kv = dot_t(flat_kv, full_kv).reshape(micros, total_rows, width)
    grad_x = (grad_sum1 + dot_t(grad_q, full_query)).reshape(micros, rows, width)
    if seqs == 2:
        grad_x = grad_x + via_kv[:, :rows]
        grad_x = grad_x + lax.ppermute(via_kv[:, rows:].astype(BF16), "seq", [(1, 0)]).astype(F32)
    else:
        grad_x = grad_x + lax.psum_scatter(via_kv, "seq", scatter_dimension=1, tiled=True)

    vec = own_first[:, 3 * width : 3 * width + small_count]
    v_of = [vec[:, i] for i in range(8)]
    outputs = result.reshape(micros, rows, width)[None]
    return (
        outputs,
        grad_x[None],
        own_first[:, :width],
        own_first[:, width : 2 * width],
        own_first[:, 2 * width : 3 * width],
        v_of[0],
        v_of[1],
        own_second[:, :width],
        v_of[2],
        v_of[3],
        v_of[4],
        own_second[:, width:],
        vec[:, 8:].reshape(own * per),
        own_outer,
        v_of[5],
        v_of[6],
        v_of[7],
    )


def solution(mesh):
    act = P("dp", None, "seq", None)
    mat = P(BOTH, None)
    vec = P(BOTH)
    params = (mat, mat, mat, vec, vec, mat, vec, vec, vec, mat, vec, mat, vec, vec, vec)
    return jax.shard_map(
        on_device,
        mesh=mesh,
        in_specs=(act,) + params + (P("dp", None), act),
        out_specs=(act, act) + params,
        check_vma=False,
    )
```

time: 1420 us -> 765 us (0.54)
  waiting for transfers between devices: 884 us -> 338 us
  blocking collectives: 82.8 us -> 0 us
  matrix products: 296 us -> 241 us
  local copies, waits for them, and re-layouts: 46.7 us -> 68.8 us
    unnamed x23 -> x7, waiting for transfers between devices: 317 us -> 15.2 us
    all_gather x10 -> x3, waiting for transfers between devices: 272 us -> 29.6 us  [the longest x1 20.3 us: on_device(): full_outer = lax.all_gather(outer_weight, BOTH, axis=0, tiled=True)]
    unnamed x2 -> x0, blocking collectives: 82.8 us -> none
    reduce_scatter x7 -> x2, waiting for transfers between devices: 295 us -> 224 us  [the longest x1 116 us: on_device(): lax.psum_scatter(jnp.concatenate([g_output, g_inner], axis=1).astype(BF16...]
    ppermute x0 -> x2, waiting for transfers between devices: none -> 69.4 us  [the longest x1 34.9 us: on_device(): lax.ppermute(via_kv[:, rows:].astype(BF16), 'seq', [(1, 0)]).astype(F32)]
    dot_general x48 -> x27, matrix products: 296 us -> 241 us  [the longest x2 43.2 us: attend_back(): jnp.einsum('qhd,khd->hqk', grad_h, heads_of(v), preferred_element_type=F32)]
    slice x1 -> x16, local copies, waits for them, and re-layouts: 0.58 us -> 23.5 us  [the longest x6 13.5 us: on_device(): mixed_m, saved_m = attend(queries[m], keys[m], values[m], key_pos, limit)]
    unnamed x224 -> x128, local copies, waits for them, and re-layouts: 31.2 us -> 8.41 us
  transfers between devices with their start and end apart: 20 -> 8, of which waited for: 17 -> 7; matrix products, arithmetic and copies ran while one was open for 24% -> 23% of each run, Pallas kernels for 0% -> 0%
where the time goes in v1:
time: 765 us; the launch traced here: 759 us
  waiting for transfers between devices  338 us (44%)
  matrix products  241 us (32%)
  other arithmetic  91 us (12%)
  local copies, waits for them, and re-layouts  68.8 us (9%)
  between operations  16.4 us (2%)
    reduce_scatter x1, waiting for transfers between devices, on_device(): lax.psum_scatter(jnp.concatenate([g_output, g_inner], axis=1).astype(BF16...  116 us
    reduce_scatter x1, waiting for transfers between devices, on_device(): lax.psum_scatter(g_outer, BOTH, scatter_dimension=0, tiled=True).astype(F32)  107 us
    dot_general x2, matrix products, attend_back(): jnp.einsum('qhd,khd->hqk', grad_h, heads_of(v), preferred_element_type=F32)  43.2 us
    dot_general x5, matrix products, dot_t(): lax.dot_general(a, b, (((1,), (1,)), ((), ())), preferred_element_type=F32)  35.8 us
    dot_general x5, matrix products, t_dot(): lax.dot_general(a, b, (((0,), (0,)), ((), ())), preferred_element_type=F32)  35.6 us
    convert_element_type x2, other arithmetic, attend_back(): grad_scores = (probs * (grad_probs - row_dot)).astype(BF16)  34.9 us
    ppermute x1, waiting for transfers between devices, on_device(): lax.ppermute(via_kv[:, rows:].astype(BF16), 'seq', [(1, 0)]).astype(F32)  34.9 us
    ppermute x1, waiting for transfers between devices, on_device(): before = lax.ppermute(x, 'seq', [(0, 1)])  34.5 us
  transfers between devices with their start and end apart: 8, of which 7 were waited for; matrix products, arithmetic and copies ran while one was open for 23% of the time, Pallas kernels for 0%

profile of v1, /device:TPU:12, one launch (start us, length us, event | category | flops | bytes accessed | tf_op | source)
XLA Modules:
  0.0 759.3 jit_solution(18443517237392561761)
XLA Ops:
  25.3 34.5 %collective-permute-done = bf16[2,512,768]{1,2,0:T(8,128)(2,1)} collective-permute-done((bf16[2,512,768]{1,2,0:T(8,128)(2,1)S(1)}, bf16[2,512,768]{1,2,0:T(8,128)(2,1)}, u32[]{:S(2)}, u32[]{:S(2)}) %collective-permute-start) | collective-permute-done | bytes 1572896 | tf_op jit(solution)/shard_map/ppermute | solution.py:103
  68.5 9.3 %all-gather.4.cloned.1.call-done = bf16[768,2432]{1,0:T(8,128)(2,1)} async-done(((bf16[24,2432]{1,0:T(8,128)(2,1)}), bf16[768,2432]{1,0:T(8,128)(2,1)}) %all-gather.4.cloned.1.call-update) | async-done | bytes 3735568 | tf_op jit(solution)/shard_map/all_gather | solution.py:120
  95.3 12.8 %fusion.1 = (f32[12,512]{1,0:T(8,128)S(1)}, f32[12,512,1024]{2,1,0:T(8,128)}) fusion(pred[512,1024]{1,0:T(8,128)(4,1)} %get-tuple-element.56, bf16[512,12,64]{0,2,1:T(8,128)(2,1)} %bitcast.115, bf16[1024,12,64]{0,2,1:T(8,128)(2,1)S(1)} %bitcast.111), kind=kOutput, calls=%fused_computation.11 | convolution fusion | flops 824174592 | bytes 28073984 | tf_op jit(solution)/shard_map/qhd,khd->hqk/dot_general | solution.py:45
  108.1 12.4 %exponential_reduce_fusion = f32[12,512]{1,0:T(8,128)} fusion(f32[12,512,1024]{2,1,0:T(8,128)} %get-tuple-element.60, f32[12,512]{1,0:T(8,128)S(1)} %get-tuple-element.59, pred[512,1024]{1,0:T(8,128)(4,1)S(1)} %copy-done.3), kind=kLoop, calls=%fused_computation.5 | loop fusion | flops 25159680 | bytes 25739264 | tf_op jit(solution)/shard_map/reduce_sum | solution.py:48
  128.7 12.3 %fusion = (f32[12,512]{1,0:T(8,128)S(1)}, f32[12,512,1024]{2,1,0:T(8,128)}) fusion(pred[512,1024]{1,0:T(8,128)(4,1)} %get-tuple-element.55, bf16[512,12,64]{0,2,1:T(8,128)(2,1)} %bitcast.117, bf16[1024,12,64]{0,2,1:T(8,128)(2,1)S(1)} %bitcast.113), kind=kOutput, calls=%fused_computation.10 | convolution fusion | flops 824174592 | bytes 28073984 | tf_op jit(solution)/shard_map/qhd,khd->hqk/dot_general | solution.py:45
  141.0 12.1 %exponential_reduce_fusion.1 = f32[12,512]{1,0:T(8,128)S(1)} fusion(f32[12,512,1024]{2,1,0:T(8,128)} %get-tuple-element.62, f32[12,512]{1,0:T(8,128)S(1)} %get-tuple-element.61, pred[512,1024]{1,0:T(8,128)(4,1)S(1)} %copy-done.7), kind=kLoop, calls=%fused_computation.8 | loop fusion | flops 25159680 | bytes 25739264 | tf_op jit(solution)/shard_map/reduce_sum | solution.py:48
  153.2 12.2 %convolution_convert_fusion.7 = bf16[12,64,512]{2,1,0:T(8,128)(2,1)} fusion(bf16[1024,12,64]{0,2,1:T(8,128)(2,1)S(1)} %bitcast.121, f32[12,512,1024]{2,1,0:T(8,128)} %get-tuple-element.60, f32[12,512]{1,0:T(8,128)S(1)} %log_add_fusion, pred[512,1024]{1,0:T(8,128)(4,1)S(1)} %copy-done.4), kind=kOutput, calls=%fused_computation.85 | convolution fusion | flops 830865408 | bytes 28073984 | tf_op jit(solution)/shard_map/hqk,khd->qhd/dot_general | solution.py:51
  165.4 11.9 %convolution_convert_fusion.8 = bf16[12,64,512]{2,1,0:T(8,128)(2,1)} fusion(bf16[1024,12,64]{0,2,1:T(8,128)(2,1)S(1)} %bitcast.123, f32[12,512,1024]{2,1,0:T(8,128)} %get-tuple-element.62, f32[12,512]{1,0:T(8,128)S(1)} %log_add_fusion.1, pred[512,1024]{1,0:T(8,128)(4,1)S(1)} %copy-done.7), kind=kOutput, calls=%fused_computation.86 | convolution fusion | flops 830865408 | bytes 28073984 | tf_op jit(solution)/shard_map/hqk,khd->qhd/dot_general | solution.py:51
  183.2 9.9 %multiply_convert_fusion.2 = (bf16[1024,3072]{1,0:T(8,128)(2,1)}, f32[1024,3072]{1,0:T(8,128)}) fusion(f32[3072]{0:T(1024)S(1)} %add.172, bf16[768,3840]{1,0:T(8,128)(2,1)S(1)} %bitcast.155, f32[1024,768]{1,0:T(8,128)S(1)} %get-tuple-element.64, f32[768]{0:T(1024)S(1)} %copy-done.50, f32[768]{0:T(1024)S(1)} %get-tuple-element.27, ...), kind=kOutput, calls=%fused_computation.21 | convolution fusion | flops 4854644736 | bytes 26767360 | tf_op jit(solution)/shard_map/dot_general | solution.py:16
  193.0 20.3 %all-gather.8.cloned.1.call-done = bf16[3072,768]{1,0:T(8,128)(2,1)} async-done(((bf16[96,768]{1,0:T(8,128)(2,1)}), bf16[3072,768]{1,0:T(8,128)(2,1)}) %all-gather.8.cloned.1.call-update) | async-done | bytes 4718608 | tf_op jit(solution)/shard_map/all_gather | solution.py:126
  213.4 9.3 %fusion.72 = (f32[1024]{0:T(1024)S(1)}, f32[1024,768]{1,0:T(8,128)S(1)}) fusion(f32[768]{0:T(1024)S(1)} %copy-done.52, bf16[1024,3072]{1,0:T(8,128)(2,1)} %get-tuple-element.65, bf16[3072,768]{1,0:T(8,128)(2,1)} %all-gather.8.cloned.1.call-done, f32[768]{0:T(1024)S(1)} %copy-done.50, f32[768]{0:T(1024)S(1)} %get-tuple-element.27, ...), kind=kOutput, calls=%fused_computation.155 | convolution fusion | flops 4837342208 | bytes 17323008 | tf_op jit(solution)/shard_map/dot_general | solution.py:16
  228.5 14.9 %fusion.73 = (bf16[3072]{0:T(1024)(128)(2,1)}, bf16[1024,3072]{1,0:T(8,128)(2,1)}) fusion(f32[1024,3072]{1,0:T(8,128)} %get-tuple-element.66, f32[3072]{0:T(1024)S(1)} %add.172, bf16[3072,768]{1,0:T(8,128)(2,1)S(1)} %bitcast.159, f32[1024,768]{1,0:T(8,128)S(1)} %get-tuple-element.40), kind=kOutput, calls=%fused_computation.156 | convolution fusion | flops 4876661760 | bytes 26757120 | tf_op jit(solution)/shard_map/dot_general | solution.py:20
  243.4 8.8 %multiply_reduce_fusion.2 = (bf16[768]{0:T(1024)(128)(2,1)}, f32[1024]{0:T(1024)S(1)}, f32[1024]{0:T(1024)S(1)}, bf16[768]{0:T(1024)(128)(2,1)}, f32[1024,768]{1,0:T(8,128)S(1)}) fusion(f32[1024,768]{1,0:T(8,128)S(1)} %copy-done.10, f32[1024]{0:T(1024)S(1)} %add_rsqrt_fusion.1, f32[1024]{0:T(1024)S(1)} %broadcast_multiply_fusion.4, ...), kind=kOutput, calls=%fused_computation.52 | convolution fusion | flops 4839698432 | bytes 20470784 | tf_op jit(solution)/shard_map/dot_general | solution.py:20
  257.1 12.7 %convolution_convert_fusion.3 = bf16[12,64,1024]{2,1,0:T(8,128)(2,1)} fusion(bf16[512,12,64]{0,2,1:T(8,128)(2,1)S(1)} %bitcast.133, f32[12,512,1024]{2,1,0:T(8,128)} %get-tuple-element.62, f32[12,512]{1,0:T(8,128)S(1)} %copy-done.40, pred[512,1024]{1,0:T(8,128)(4,1)S(1)} %copy-done.8), kind=kOutput, calls=%fused_computation.75 | convolution fusion | flops 831258624 | bytes 28073984 | tf_op jit(solution)/shard_map/hqk,qhd->khd/dot_general | solution.py:63
  269.8 21.9 %multiply_reduce_fusion.1 = (f32[12,512]{1,0:T(8,128)}, f32[12,512,1024]{2,1,0:T(8,128)}) fusion(f32[12,512,1024]{2,1,0:T(8,128)} %get-tuple-element.62, f32[12,512]{1,0:T(8,128)S(1)} %copy-done.40, pred[512,1024]{1,0:T(8,128)(4,1)S(1)} %copy-done.8, bf16[512,12,64]{0,2,1:T(8,128)(2,1)S(1)} %bitcast.134, bf16[1024,12,64]{0,2,1:T(8,128)(2,1)S(1)} %bitcast.124), kind=kOutput, calls=%fused_computation.3 | convolution fusion | flops 836757504 | bytes 53264384 | tf_op jit(solution)/shard_map/qhd,khd->hqk/dot_general | solution.py:58
  291.7 17.5 %multiply_convert_fusion.1 = bf16[12,512,1024]{2,1,0:T(8,128)(2,1)S(1)} fusion(f32[12,512,1024]{2,1,0:T(8,128)} %get-tuple-element.73, f32[12,512,1024]{2,1,0:T(8,128)} %get-tuple-element.62, f32[12,512]{1,0:T(8,128)} %get-tuple-element.72, f32[12,512]{1,0:T(8,128)} %copy-done.39, pred[512,1024]{1,0:T(8,128)(4,1)} %get-tuple-element.55), kind=kLoop, calls=%fused_computation.2 | loop fusion | flops 37748736 | bytes 63488000 | tf_op jit(solution)/shard_map/convert_element_type | solution.py:60
  320.2 12.8 %convolution_convert_fusion.2 = bf16[12,64,1024]{2,1,0:T(8,128)(2,1)} fusion(bf16[512,12,64]{0,2,1:T(8,128)(2,1)S(1)} %bitcast.131, f32[12,512,1024]{2,1,0:T(8,128)} %get-tuple-element.60, f32[12,512]{1,0:T(8,128)S(1)} %copy-done.38, pred[512,1024]{1,0:T(8,128)(4,1)S(1)} %copy-done.5), kind=kOutput, calls=%fused_computation.74 | convolution fusion | flops 831258624 | bytes 28073984 | tf_op jit(solution)/shard_map/hqk,qhd->khd/dot_general | solution.py:63
  333.0 21.3 %multiply_reduce_fusion = (f32[12,512]{1,0:T(8,128)S(1)}, f32[12,512,1024]{2,1,0:T(8,128)}) fusion(f32[12,512,1024]{2,1,0:T(8,128)} %get-tuple-element.60, f32[12,512]{1,0:T(8,128)S(1)} %copy-done.38, pred[512,1024]{1,0:T(8,128)(4,1)S(1)} %copy-done.6, bf16[512,12,64]{0,2,1:T(8,128)(2,1)S(1)} %bitcast.132, bf16[1024,12,64]{0,2,1:T(8,128)(2,1)S(1)} %bitcast.122), kind=kOutput, calls=%fused_computation.1 | convolution fusion | flops 836757504 | bytes 53264384 | tf_op jit(solution)/shard_map/qhd,khd->hqk/dot_general | solution.py:58
  354.3 17.4 %multiply_convert_fusion = bf16[12,512,1024]{2,1,0:T(8,128)(2,1)S(1)} fusion(f32[12,512,1024]{2,1,0:T(8,128)} %get-tuple-element.71, f32[12,512,1024]{2,1,0:T(8,128)} %get-tuple-element.60, f32[12,512]{1,0:T(8,128)S(1)} %get-tuple-element.70, f32[12,512]{1,0:T(8,128)S(1)} %copy-done.38, pred[512,1024]{1,0:T(8,128)(4,1)} %get-tuple-element.56), kind=kLoop, calls=%fused_computation | loop fusion | flops 37748736 | bytes 63488000 | tf_op jit(solution)/shard_map/convert_element_type | solution.py:60
  422.3 9.9 %convolution_convert_fusion = bf16[3072,768]{1,0:T(8,128)(2,1)} fusion(bf16[1024,3072]{1,0:T(8,128)(2,1)} %get-tuple-element.65, f32[1024,768]{1,0:T(8,128)S(1)} %copy-done.28), kind=kOutput, calls=%fused_computation.28 | convolution fusion | flops 4834983936 | bytes 14155776 | tf_op jit(solution)/shard_map/dot_general | solution.py:24
  467.0 34.9 %collective-permute-done.1 = bf16[2,512,768]{2,1,0:T(8,128)(2,1)S(1)} collective-permute-done((bf16[2,512,768]{2,1,0:T(8,128)(2,1)S(1)}, bf16[2,512,768]{2,1,0:T(8,128)(2,1)S(1)}, u32[]{:S(2)}, u32[]{:S(2)}) %collective-permute-start.1) | collective-permute-done | bytes 1572896 | tf_op jit(solution)/shard_map/ppermute | solution.py:213
  504.2 15.2 %reduce-scatter.10.cloned.1.call-done = bf16[24,2432]{1,0:T(8,128)(2,1)} async-done(((bf16[768,2432]{1,0:T(8,128)(2,1)}), bf16[24,2432]{1,0:T(8,128)(2,1)}) %reduce-scatter.10.cloned.1.call-update) | async-done | bytes 116752
  524.0 107.4 %reduce-scatter.8.cloned.1.call-done = bf16[96,768]{1,0:T(8,128)(2,1)} async-done(((bf16[3072,768]{1,0:T(8,128)(2,1)}), bf16[96,768]{1,0:T(8,128)(2,1)}) %reduce-scatter.8.cloned.1.call-update) | async-done | bytes 147472 | tf_op jit(solution)/shard_map/reduce_scatter | solution.py:165
  633.0 116.2 %reduce-scatter.6.cloned.1.call-done = bf16[24,3840]{1,0:T(8,128)(2,1)} async-done(((bf16[768,3840]{1,0:T(8,128)(2,1)}), bf16[24,3840]{1,0:T(8,128)(2,1)}) %reduce-scatter.6.cloned.1.call-update) | async-done | bytes 184336 | tf_op jit(solution)/shard_map/reduce_scatter | solution.py:177
  (240 shorter events, 174.9 us)
Async XLA Ops:
  7.2 13.4 %copy-start.56 = (s32[1,2]{1,0:T(1,128)S(1)}, s32[1,2]{1,0:T(1,128)}, u32[]{:S(2)}) copy-start(s32[1,2]{1,0:T(1,128)} %param.34) | copy-start | bytes 28
  7.2 15.2 %copy-start = (bf16[1,2,512,768]{3,2,1,0:T(8,128)(2,1)S(1)}, bf16[1,2,512,768]{3,2,1,0:T(8,128)(2,1)}, u32[]{:S(2)}) copy-start(bf16[1,2,512,768]{3,2,1,0:T(8,128)(2,1)} %param.35) | copy-start | bytes 4718596
  7.2 70.6 %all-gather.4.cloned.1.call-start = ((), (), s32[]{:S(2)}) async-start(), calls=%async_computation.3 | async-start | bytes 3852288 | tf_op jit(solution)/shard_map/all_gather | solution.py:120
  15.7 161.7 %all-gather.6.cloned.1.call-start = ((), (), s32[]{:S(2)}) async-start(), calls=%async_computation.4 | async-start | bytes 6082560 | tf_op jit(solution)/shard_map/all_gather | solution.py:123
  17.4 196.0 %all-gather.8.cloned.1.call-start = ((), (), s32[]{:S(2)}) async-start(), calls=%async_computation.5 | async-start | bytes 4866048 | tf_op jit(solution)/shard_map/all_gather | solution.py:126
  19.1 44.2 %copy-start.21 = (bf16[1,2,512,768]{2,3,1,0:T(8,128)(2,1)}, bf16[1,2,512,768]{2,3,1,0:T(8,128)(2,1)S(1)}, u32[]{:S(2)}) copy-start(bf16[1,2,512,768]{2,3,1,0:T(8,128)(2,1)S(1)} %copy.104) | copy-start | bytes 4718596
  19.2 40.6 %collective-permute-start = (bf16[2,512,768]{1,2,0:T(8,128)(2,1)S(1)}, bf16[2,512,768]{1,2,0:T(8,128)(2,1)}, u32[]{:S(2)}, u32[]{:S(2)}) collective-permute-start(bf16[2,512,768]{1,2,0:T(8,128)(2,1)S(1)} %bitcast.126), channel_id=1, source_target_pairs={{0,16},{1,17},{2,18},{3,19},{4,20},{5,21},{6,22},{7,23},{8,24},{9,... | collective-permute-start | bytes 4718600 | tf_op jit(solution)/shard_map/ppermute | solution.py:103
  20.5 498.9 %reduce-scatter.10.cloned.1.call-start = ((), (), s32[]{:S(2)}) async-start(), calls=%async_computation.8 | async-start | bytes 3852288
  68.5 12.8 %copy-start.31 = (bf16[1,2,512,768]{3,2,1,0:T(8,128)(2,1)S(1)}, bf16[1,2,512,768]{3,2,1,0:T(8,128)(2,1)}, u32[]{:S(2)}) copy-start(bf16[1,2,512,768]{3,2,1,0:T(8,128)(2,1)} %param.18) | copy-start | bytes 4718596
  95.3 12.8 %copy-start.1 = (bf16[1,1024,768]{1,2,0:T(8,128)(2,1)}, bf16[1,1024,768]{1,2,0:T(8,128)(2,1)S(1)}, u32[]{:S(2)}) copy-start(bf16[1,1024,768]{1,2,0:T(8,128)(2,1)S(1)} %copy.117) | copy-start | bytes 4718596
  95.3 12.8 %copy-start.3 = (pred[512,1024]{1,0:T(8,128)(4,1)S(1)}, pred[512,1024]{1,0:T(8,128)(4,1)}, u32[]{:S(2)}) copy-start(pred[512,1024]{1,0:T(8,128)(4,1)} %get-tuple-element.56) | copy-start | bytes 1572868
  108.1 12.4 %copy-start.41 = (f32[12,512]{1,0:T(8,128)}, f32[12,512]{1,0:T(8,128)S(1)}, u32[]{:S(2)}) copy-start(f32[12,512]{1,0:T(8,128)S(1)} %get-tuple-element.59) | copy-start | bytes 73732
  128.6 24.5 %copy-start.37 = (f32[12,512]{1,0:T(8,128)}, f32[12,512]{1,0:T(8,128)S(1)}, u32[]{:S(2)}) copy-start(f32[12,512]{1,0:T(8,128)S(1)} %log_add_fusion) | copy-start | bytes 73732
  183.2 30.2 %copy-start.52 = (f32[768]{0:T(1024)S(1)}, f32[768]{0:T(1024)}, u32[]{:S(2)}) copy-start(f32[768]{0:T(1024)} %get-tuple-element.25) | copy-start | bytes 9220
  226.7 16.7 %slice-start.2 = ((s8[5898240]{0:T(1024)(128)(4,1)}), s8[4194304]{0:T(1024)(128)(4,1)S(1)}, s32[]{:S(2)}) async-start(s8[5898240]{0:T(1024)(128)(4,1)} %bitcast.156), calls=%async_computation.11 | async-start | bytes 8388608
  228.4 15.0 %copy-start.27 = (f32[1024,768]{1,0:T(8,128)}, f32[1024,768]{1,0:T(8,128)S(1)}, u32[]{:S(2)}) copy-start(f32[1024,768]{1,0:T(8,128)S(1)} %get-tuple-element.40) | copy-start | bytes 9437188
  228.4 14.9 %copy-start.10 = (f32[1024,768]{1,0:T(8,128)S(1)}, f32[1024,768]{1,0:T(8,128)}, u32[]{:S(2)}) copy-start(f32[1024,768]{1,0:T(8,128)} %copy-done.9) | copy-start | bytes 9437188
  228.5 14.9 %slice-start.3 = ((s8[5898240]{0:T(1024)(128)(4,1)}), s8[1703936]{0:T(1024)(128)(4,1)S(1)}, s32[]{:S(2)}) async-start(s8[5898240]{0:T(1024)(128)(4,1)} %bitcast.156), calls=%async_computation.12 | async-start | bytes 3407872
  320.1 12.9 %copy-start.6 = (pred[512,1024]{1,0:T(8,128)(4,1)S(1)}, pred[512,1024]{1,0:T(8,128)(4,1)}, u32[]{:S(2)}) copy-start(pred[512,1024]{1,0:T(8,128)(4,1)} %get-tuple-element.56) | copy-start | bytes 1572868
  320.1 12.9 %copy-start.15 = (bf16[1,1024,768]{1,2,0:T(8,128)(2,1)S(1)}, bf16[1,1024,768]{1,2,0:T(8,128)(2,1)}, u32[]{:S(2)}) copy-start(bf16[1,1024,768]{1,2,0:T(8,128)(2,1)} %copy.116) | copy-start | bytes 4718596
  320.1 12.9 %copy-start.30 = (bf16[512,768]{0,1:T(8,128)(2,1)S(1)}, bf16[512,768]{0,1:T(8,128)(2,1)}, u32[]{:S(2)}) copy-start(bf16[512,768]{0,1:T(8,128)(2,1)} %get-tuple-element.49) | copy-start | bytes 2359300
  420.5 210.9 %reduce-scatter.8.cloned.1.call-start = ((), (), s32[]{:S(2)}) async-start(), calls=%async_computation.7 | async-start | bytes 4866048 | tf_op jit(solution)/shard_map/reduce_scatter | solution.py:165
  432.3 316.9 %reduce-scatter.6.cloned.1.call-start = ((), (), s32[]{:S(2)}) async-start(), calls=%async_computation.6 | async-start | bytes 6082560 | tf_op jit(solution)/shard_map/reduce_scatter | solution.py:177
  461.7 40.2 %collective-permute-start.1 = (bf16[2,512,768]{2,1,0:T(8,128)(2,1)S(1)}, bf16[2,512,768]{2,1,0:T(8,128)(2,1)S(1)}, u32[]{:S(2)}, u32[]{:S(2)}) collective-permute-start(bf16[2,512,768]{2,1,0:T(8,128)(2,1)S(1)} %slice.274), channel_id=1, source_target_pairs={{16,0},{17,1},{18,2},{19,3},{20,4},{21,5},{22,6},{23,7},{24,8},{25... | collective-permute-start | bytes 4718600 | tf_op jit(solution)/shard_map/ppermute | solution.py:213
  (47 other events, 281.1 us)
Sparse Core Ops, SparseCore 0:
  15.8 61.9 all-gather.3
  81.3 67.1 all-gather.5
  151.4 61.9 all-gather.7
  420.6 98.7 reduce-scatter.9
  524.7 106.6 reduce-scatter.7
  636.9 112.3 reduce-scatter.5

commit v2 on v1

--- a/solution.py
+++ b/solution.py
@@ -1,6 +1,10 @@
+import functools
+
 import jax
 import jax.numpy as jnp
 from jax import lax
+from jax.experimental import pallas as pl
+from jax.experimental.pallas import tpu as pltpu
 from jax.sharding import PartitionSpec as P
 
 HEADS = 12
@@ -10,6 +14,257 @@
 BOTH = ("seq", "dp")
 F32 = jnp.float32
 BF16 = jnp.bfloat16
+MESH = pl.DeviceIdType.MESH
+RING = 16
+FW = 8
+BW = 7
+
+
+def ring_place():
+    y, dp = lax.axis_index("seq"), lax.axis_index("dp")
+    z, x, core = dp // 4, (dp // 2) % 2, dp % 2
+    column = 2 * x + (x + y) % 2
+    return 4 * column + jnp.where(column % 2 == 0, z, 3 - z), core
+
+
+def ring_coords(t, core):
+    column, k = t // 4, t % 4
+    z = jnp.where(column % 2 == 0, k, 3 - k)
+    return ((column + 1) // 2) % 2, 4 * z + 2 * (column // 2) + core
+
+
+def ring_device(t, core):
+    y, dp = ring_coords(t, core)
+    return y * RING + dp
+
+
+def meet(targets):
+    barrier = pltpu.get_barrier_semaphore()
+    for target in targets:
+        pl.semaphore_signal(barrier, inc=1, device_id=target, device_id_type=MESH)
+    pl.semaphore_wait(barrier, len(targets))
+
+
+def remote(src, dst, send, recv, target):
+    return pltpu.make_async_remote_copy(
+        src_ref=src, dst_ref=dst, send_sem=send, recv_sem=recv, device_id=target, device_id_type=MESH
+    )
+
+
+def scatter_kernel(count, *refs):
+    g, out = refs[:count], refs[count : 2 * count]
+    own, pair, fw, bw = [refs[(2 + i) * count : (3 + i) * count] for i in range(4)]
+    local_sem, pair_send, pair_recv, fw_send, fw_recv, bw_send, bw_recv = refs[6 * count :]
+    r, core = ring_place()
+    after, before = (r + 1) % RING, (r + RING - 1) % RING
+    right, left, partner = ring_coords(after, core), ring_coords(before, core), ring_coords(r, 1 - core)
+
+    def local(k, t):
+        return pltpu.make_async_copy(g[k].at[ring_device(t, core)], own[k].at[t], local_sem.at[k, t])
+
+    def to_pair(k, t):
+        return remote(
+            g[k].at[ring_device(t, 1 - core)], pair[k].at[t], pair_send.at[k, t], pair_recv.at[k, t], partner
+        )
+
+    def forth(k, h, src):
+        return remote(src, fw[k].at[h], fw_send.at[k, h], fw_recv.at[k, h], right)
+
+    def back(k, h, src):
+        return remote(src, bw[k].at[h], bw_send.at[k, h], bw_recv.at[k, h], left)
+
+    def term(k, t):
+        local(k, t).wait()
+        to_pair(k, t).wait_recv()
+        return own[k][t].astype(F32) + pair[k][t].astype(F32)
+
+    meet((right, left, partner))
+
+    def begin(i, _):
+        t = (r + jnp.where(i % 2 == 0, FW - i // 2, FW + 1 + i // 2)) % RING
+        for k in range(count):
+            to_pair(k, t).start()
+            local(k, t).start()
+        return 0
+
+    lax.fori_loop(0, RING, begin, 0)
+
+    for k in range(count):
+        t = (r + FW) % RING
+        pair[k][t] = term(k, t).astype(BF16)
+        forth(k, 0, pair[k].at[t]).start()
+        t = (r + RING - BW) % RING
+        pair[k][t] = term(k, t).astype(BF16)
+        back(k, 0, pair[k].at[t]).start()
+
+    def forth_step(k, h):
+        t = (r + FW - h) % RING
+        mine = term(k, t)
+        forth(k, h - 1, pair[k].at[t]).wait_recv()
+        fw[k][h - 1] = (fw[k][h - 1].astype(F32) + mine).astype(BF16)
+        forth(k, h, fw[k].at[h - 1]).start()
+
+    def back_step(k, h):
+        t = (r + RING - BW + h) % RING
+        mine = term(k, t)
+        back(k, h - 1, pair[k].at[t]).wait_recv()
+        bw[k][h - 1] = (bw[k][h - 1].astype(F32) + mine).astype(BF16)
+        back(k, h, bw[k].at[h - 1]).start()
+
+    def hop(h, _):
+        for k in range(count):
+            forth_step(k, h)
+            back_step(k, h)
+        return 0
+
+    lax.fori_loop(1, BW, hop, 0)
+    for k in range(count):
+        forth_step(k, FW - 1)
+    for k in range(count):
+        mine = term(k, r)
+        back(k, BW - 1, pair[k].at[r]).wait_recv()
+        mine = mine + bw[k][BW - 1].astype(F32)
+        forth(k, FW - 1, pair[k].at[r]).wait_recv()
+        out[k][...] = mine + fw[k][FW - 1].astype(F32)
+
+    def drain(i, _):
+        for k in range(count):
+            to_pair(k, i).wait_send()
+        return 0
+
+    lax.fori_loop(0, RING, drain, 0)
+    for k in range(count):
+        for h in range(FW):
+            forth(k, h, pair[k].at[0]).wait_send()
+        for h in range(BW):
+            back(k, h, pair[k].at[0]).wait_send()
+
+
+def ring_scatter(parts, collective_id):
+    count = len(parts)
+    slots = lambda n: [pltpu.VMEM((n,) + p.shape[1:], BF16) for p in parts]
+    dma = lambda n: pltpu.SemaphoreType.DMA((count, n))
+    return pl.pallas_call(
+        functools.partial(scatter_kernel, count),
+        out_shape=[jax.ShapeDtypeStruct(p.shape[1:], F32) for p in parts],
+        in_specs=[pl.BlockSpec(memory_space=pl.ANY)] * count,
+        out_specs=[pl.BlockSpec(memory_space=pltpu.VMEM)] * count,
+        scratch_shapes=slots(RING) + slots(RING) + slots(FW) + slots(BW)
+        + [dma(RING), dma(RING), dma(RING), dma(FW), dma(FW), dma(BW), dma(BW)],
+        compiler_params=pltpu.CompilerParams(
+            collective_id=collective_id, has_side_effects=True, vmem_limit_bytes=60 * 2**20
+        ),
+        name="ring_scatter",
+    )(*parts)
+
+
+def gather_kernel(count, *refs):
+    s, o = refs[:count], refs[count : 2 * count]
+    local_sem, pair_send, pair_recv, fw_send, fw_recv, bw_send, bw_recv = refs[2 * count :]
+    r, core = ring_place()
+    after, before = (r + 1) % RING, (r + RING - 1) % RING
+    right, left, partner = ring_coords(after, core), ring_coords(before, core), ring_coords(r, 1 - core)
+
+    def place(k, t):
+        return o[k].at[ring_device(t, core)]
+
+    def local(k):
+        return pltpu.make_async_copy(s[k], place(k, r), local_sem.at[k])
+
+    def to_pair(k, t, src):
+        return remote(src, place(k, t), pair_send.at[k, t], pair_recv.at[k, t], partner)
+
+    def forth(k, h, t, src):
+        return remote(src, place(k, t), fw_send.at[k, h], fw_recv.at[k, h], right)
+
+    def back(k, h, t, src):
+        return remote(src, place(k, t), bw_send.at[k, h], bw_recv.at[k, h], left)
+
+    meet((right, left, partner))
+    for k in range(count):
+        forth(k, 0, r, s[k]).start()
+        back(k, 0, r, s[k]).start()
+        to_pair(k, r, s[k]).start()
+        local(k).start()
+
+    def forth_step(k, h):
+        t = (r + RING - h) % RING
+        forth(k, h - 1, t, place(k, t)).wait_recv()
+        return t
+
+    def back_step(k, h):
+        t = (r + h) % RING
+        back(k, h - 1, t, place(k, t)).wait_recv()
+        return t
+
+    def hop(h, _):
+        for k in range(count):
+            t = forth_step(k, h)
+            forth(k, h, t, place(k, t)).start()
+            to_pair(k, t, place(k, t)).start()
+            t = back_step(k, h)
+            back(k, h, t, place(k, t)).start()
+            to_pair(k, t, place(k, t)).start()
+        return 0
+
+    lax.fori_loop(1, BW, hop, 0)
+    for k in range(count):
+        t = forth_step(k, FW - 1)
+        forth(k, FW - 1, t, place(k, t)).start()
+        to_pair(k, t, place(k, t)).start()
+        t = back_step(k, BW)
+        to_pair(k, t, place(k, t)).start()
+    for k in range(count):
+        t = forth_step(k, FW)
+        to_pair(k, t, place(k, t)).start()
+
+    def drain(t, _):
+        for k in range(count):
+            copy = to_pair(k, t, place(k, t))
+            copy.wait_send()
+            copy.wait_recv()
+        return 0
+
+    lax.fori_loop(0, RING, drain, 0)
+    for k in range(count):
+        local(k).wait()
+        for h in range(FW):
+            forth(k, h, r, s[k]).wait_send()
+        for h in range(BW):
+            back(k, h, r, s[k]).wait_send()
+
+
+def ring_gather(parts, collective_id):
+    count = len(parts)
+    dma = lambda n: pltpu.SemaphoreType.DMA((count, n))
+    return pl.pallas_call(
+        functools.partial(gather_kernel, count),
+        out_shape=[jax.ShapeDtypeStruct((2 * RING,) + p.shape, p.dtype) for p in parts],
+        in_specs=[pl.BlockSpec(memory_space=pltpu.VMEM)] * count,
+        out_specs=[pl.BlockSpec(memory_space=pl.ANY)] * count,
+        scratch_shapes=[pltpu.SemaphoreType.DMA((count,))]
+        + [dma(RING), dma(RING), dma(FW), dma(FW), dma(BW), dma(BW)],
+        compiler_params=pltpu.CompilerParams(collective_id=collective_id, has_side_effects=True),
+        name="ring_gather",
+    )(*parts)
+
+
+def use_ring():
+    return lax.axis_size("seq") == 2 and lax.axis_size("dp") == RING
+
+
+def gather_all(parts, collective_id):
+    if use_ring():
+        full = ring_gather(parts, collective_id)
+        return [f.reshape((-1,) + f.shape[2:]) for f in full]
+    return [lax.all_gather(p, BOTH, axis=0, tiled=True) for p in parts]
+
+
+def scatter_all(parts, collective_id):
+    if use_ring():
+        split = [p.astype(BF16).reshape(2 * RING, -1, p.shape[1]) for p in parts]
+        return ring_scatter(split, collective_id)
+    return [lax.psum_scatter(p.astype(BF16), BOTH, scatter_dimension=0, tiled=True).astype(F32) for p in parts]
 
 
 def dot(a, b):
@@ -112,30 +367,20 @@
     flat_key_x = key_x.reshape(micros * total_rows, width)
 
     vectors = (query_bias, value_bias, output_bias, first_gain, first_shift, outer_bias, second_gain, second_shift)
-    small = jnp.concatenate(
-        [jnp.stack(vectors, axis=1), inner_bias.reshape(own, per)], axis=1
-    )
+    small = jnp.concatenate([jnp.stack(vectors, axis=1), inner_bias.reshape(own, per)], axis=1)
     small_count = small.shape[1]
     small = jnp.pad(small, ((0, 0), (0, 128 - small_count)))
-    first_pack = lax.all_gather(
-        jnp.concatenate([query_weight, key_weight, value_weight, small], axis=1), BOTH, axis=0, tiled=True
-    )
-    second_pack = lax.all_gather(
-        jnp.concatenate([output_weight, inner_weight], axis=1), BOTH, axis=0, tiled=True
-    )
-    full_outer = lax.all_gather(outer_weight, BOTH, axis=0, tiled=True)
-    full_query = first_pack[:, :width]
-    full_kv = first_pack[:, width : 3 * width]
-    small_all = first_pack[:, 3 * width : 3 * width + small_count].astype(F32)
+    full_query, full_key, full_value, small_all = gather_all([query_weight, key_weight, value_weight, small], 1)
+    full_output, full_inner, full_outer = [
+        lax.all_gather(w, BOTH, axis=0, tiled=True) for w in (output_weight, inner_weight, outer_weight)
+    ]
+    small_all = small_all[:, :small_count].astype(F32)
     qb, vb, ob, fg, fs, ub, sg, ss = [small_all[:, i] for i in range(8)]
     ib = small_all[:, 8:].reshape(hidden_width)
-    full_output = second_pack[:, :width]
-    full_inner = second_pack[:, width:]
 
     queries = (dot(flat_x, full_query) + qb).astype(BF16).reshape(micros, rows, width)
-    kv_bias = jnp.concatenate([jnp.zeros_like(vb), vb])
-    keys_values = (dot(flat_key_x, full_kv) + kv_bias).astype(BF16).reshape(micros, total_rows, 2 * width)
-    keys, values = keys_values[..., :width], keys_values[..., width:]
+    keys = dot(flat_key_x, full_key).astype(BF16).reshape(micros, total_rows, width)
+    values = (dot(flat_key_x, full_value) + vb).astype(BF16).reshape(micros, total_rows, width)
 
     mixed_parts, saved = [], []
     for m in range(micros):
@@ -162,7 +407,6 @@
     grad_outer = grad_mid2.astype(BF16)
     g_ubias = jnp.sum(grad_outer.astype(F32), axis=0)
     g_outer = t_dot(hidden, grad_outer).astype(BF16)
-    own_outer = lax.psum_scatter(g_outer, BOTH, scatter_dimension=0, tiled=True).astype(F32)
     grad_hidden = dot_t(grad_outer, full_outer).astype(BF16)
     grad_inner = (grad_hidden.astype(F32) * slope).astype(BF16)
     g_ibias = jnp.sum(grad_inner.astype(F32), axis=0)
@@ -174,9 +418,6 @@
     grad_branch = grad_sum1.astype(BF16)
     g_obias = jnp.sum(grad_branch.astype(F32), axis=0)
     g_output = t_dot(mixed, grad_branch)
-    own_second = lax.psum_scatter(
-        jnp.concatenate([g_output, g_inner], axis=1).astype(BF16), BOTH, scatter_dimension=0, tiled=True
-    ).astype(F32)
     grad_mixed = dot_t(grad_branch, full_output).astype(BF16).reshape(micros, rows, width)
 
     gq_parts, gk_parts, gv_parts = [], [], []
@@ -188,12 +429,13 @@
         gk_parts.append(gk)
         gv_parts.append(gv)
     grad_q = jnp.concatenate(gq_parts, axis=0)
-    grad_kv = jnp.concatenate([jnp.stack(gk_parts), jnp.stack(gv_parts)], axis=-1)
-    flat_kv = grad_kv.reshape(micros * total_rows, 2 * width)
+    grad_k = jnp.stack(gk_parts).reshape(micros * total_rows, width)
+    grad_v = jnp.stack(gv_parts).reshape(micros * total_rows, width)
     g_qbias = jnp.sum(grad_q.astype(F32), axis=0)
-    g_vbias = jnp.sum(flat_kv[:, width:].astype(F32), axis=0)
+    g_vbias = jnp.sum(grad_v.astype(F32), axis=0)
     g_query = t_dot(flat_x, grad_q)
-    g_kv = t_dot(flat_key_x, flat_kv)
+    g_key = t_dot(flat_key_x, grad_k)
+    g_value = t_dot(flat_key_x, grad_v)
     g_small = jnp.concatenate(
         [
             jnp.stack([g_qbias, g_vbias, g_obias, g_fgain, g_fshift, g_ubias, g_sgain, g_sshift], axis=1),
@@ -202,11 +444,10 @@
         axis=1,
     )
     g_small = jnp.pad(g_small, ((0, 0), (0, 128 - small_count)))
-    own_first = lax.psum_scatter(
-        jnp.concatenate([g_query, g_kv, g_small], axis=1).astype(BF16), BOTH, scatter_dimension=0, tiled=True
-    ).astype(F32)
-
-    via_kv = dot_t(flat_kv, full_kv).reshape(micros, total_rows, width)
+    own_grads = scatter_all([g_outer, g_inner, g_output, g_query, g_key, g_value, g_small], 3)
+    own_outer, own_inner, own_output, own_query, own_key, own_value, own_small = own_grads
+
+    via_kv = (dot_t(grad_k, full_key) + dot_t(grad_v, full_value)).reshape(micros, total_rows, width)
     grad_x = (grad_sum1 + dot_t(grad_q, full_query)).reshape(micros, rows, width)
     if seqs == 2:
         grad_x = grad_x + via_kv[:, :rows]
@@ -214,22 +455,22 @@
     else:
         grad_x = grad_x + lax.psum_scatter(via_kv, "seq", scatter_dimension=1, tiled=True)
 
-    vec = own_first[:, 3 * width : 3 * width + small_count]
+    vec = own_small[:, :small_count]
     v_of = [vec[:, i] for i in range(8)]
     outputs = result.reshape(micros, rows, width)[None]
     return (
         outputs,
         grad_x[None],
-        own_first[:, :width],
-        own_first[:, width : 2 * width],
-        own_first[:, 2 * width : 3 * width],
+        own_query,
+        own_key,
+        own_value,
         v_of[0],
         v_of[1],
-        own_second[:, :width],
+        own_output,
         v_of[2],
         v_of[3],
         v_of[4],
-        own_second[:, width:],
+        own_inner,
         vec[:, 8:].reshape(own * per),
         own_outer,
         v_of[5],

time: 765 us -> 555 us (0.73)
  the two profiles are of different devices: /device:TPU:12 before, /device:TPU:26 now
where the time goes in v2:
time: 555 us; the launch traced here: 545 us
  matrix products  235 us (42%)
  Pallas kernels  169 us (30%)
  other arithmetic  77.6 us (14%)
  local copies, waits for them, and re-layouts  38.7 us (7%)
  between operations  16.6 us (3%)
  starting transfers between devices  6.61 us (1%)
    pallas_call x1, Pallas kernels, ring_scatter(): pl.pallas_call(functools.partial(scatter_kernel, count), out_shape=[jax.S...  103 us
    pallas_call x1, Pallas kernels, ring_gather(): pl.pallas_call(functools.partial(gather_kernel, count), out_shape=[jax.Sh...  65.3 us
    dot_general x2, matrix products, attend_back(): jnp.einsum('qhd,khd->hqk', grad_h, heads_of(v), preferred_element_type=F32)  42.6 us
    dot_general x6, matrix products, dot(): return jnp.dot(a, b, preferred_element_type=F32)  36.1 us
    convert_element_type x2, other arithmetic, attend_back(): grad_scores = (probs * (grad_probs - row_dot)).astype(BF16)  34.4 us
    dot_general x6, matrix products, t_dot(): lax.dot_general(a, b, (((0,), (0,)), ((), ())), preferred_element_type=F32)  32 us
    dot_general x6, matrix products, dot_t(): lax.dot_general(a, b, (((1,), (1,)), ((), ())), preferred_element_type=F32)  29.4 us
    dot_general x2, matrix products, attend_back(): gv = jnp.einsum('hqk,qhd->khd', low, grad_h, preferred_element_type=F32)  26.4 us
  transfers between devices with their start and end apart: 5, of which 0 were waited for; matrix products, arithmetic and copies ran while one was open for 26% of the time, Pallas kernels for 31%

profile of v2, /device:TPU:26, one launch (start us, length us, event | category | flops | bytes accessed | tf_op | source)
XLA Modules:
  0.0 545.1 jit_solution(16935019420645961157)
XLA Ops:
  17.8 65.3 %ring_gather.1 = (bf16[32,24,768]{2,1,0:T(8,128)(2,1)}, bf16[32,24,768]{2,1,0:T(8,128)(2,1)}, bf16[32,24,768]{2,1,0:T(8,128)(2,1)}, bf16[32,24,128]{2,1,0:T(8,128)(2,1)}) custom-call(bf16[24,768]{1,0:T(8,128)(2,1)} %refs_0_.1, bf16[24,768]{1,0:T(8,128)(2,1)} %refs_1_.1, bf16[24,768]{1,0:T(8,128)(2,1)} %refs_2_.1, bf16[24,128]{1,0:T(8,128)(2,1)} %pad.9.refs_3_), custom_call_target="tpu_custom_call" | custom-call | tf_op jit(solution)/shard_map/ring_gather/pallas_call | solution.py:240
  108.0 11.1 %fusion.1 = (f32[12,512]{1,0:T(8,128)S(1)}, f32[12,512,1024]{2,1,0:T(8,128)}) fusion(pred[512,1024]{1,0:T(8,128)(4,1)S(1)} %get-tuple-element.75, bf16[512,12,64]{0,2,1:T(8,128)(2,1)S(1)} %bitcast.141, bf16[1024,12,64]{0,2,1:T(8,128)(2,1)S(1)} %bitcast.137), kind=kOutput, calls=%fused_computation.11 | convolution fusion | flops 824174592 | bytes 28073984 | tf_op jit(solution)/shard_map/qhd,khd->hqk/dot_general | solution.py:300
  119.1 12.1 %exponential_reduce_fusion = f32[12,512]{1,0:T(8,128)S(1)} fusion(f32[12,512,1024]{2,1,0:T(8,128)} %get-tuple-element.79, f32[12,512]{1,0:T(8,128)S(1)} %get-tuple-element.78, pred[512,1024]{1,0:T(8,128)(4,1)S(1)} %get-tuple-element.75), kind=kLoop, calls=%fused_computation.5 | loop fusion | flops 25159680 | bytes 25739264 | tf_op jit(solution)/shard_map/reduce_sum | solution.py:303
  131.2 11.1 %fusion = (f32[12,512]{1,0:T(8,128)S(1)}, f32[12,512,1024]{2,1,0:T(8,128)}) fusion(pred[512,1024]{1,0:T(8,128)(4,1)S(1)} %get-tuple-element.74, bf16[512,12,64]{0,2,1:T(8,128)(2,1)S(1)} %bitcast.144, bf16[1024,12,64]{0,2,1:T(8,128)(2,1)S(1)} %bitcast.139), kind=kOutput, calls=%fused_computation.10 | convolution fusion | flops 824174592 | bytes 28073984 | tf_op jit(solution)/shard_map/qhd,khd->hqk/dot_general | solution.py:300
  142.4 12.2 %exponential_reduce_fusion.1 = f32[12,512]{1,0:T(8,128)S(1)} fusion(f32[12,512,1024]{2,1,0:T(8,128)} %get-tuple-element.81, f32[12,512]{1,0:T(8,128)S(1)} %get-tuple-element.80, pred[512,1024]{1,0:T(8,128)(4,1)S(1)} %get-tuple-element.74), kind=kLoop, calls=%fused_computation.8 | loop fusion | flops 25159680 | bytes 25739264 | tf_op jit(solution)/shard_map/reduce_sum | solution.py:303
  158.0 12.3 %convolution_convert_fusion.8 = bf16[12,64,512]{2,1,0:T(8,128)(2,1)S(1)} fusion(bf16[1024,12,64]{0,2,1:T(8,128)(2,1)S(1)} %bitcast.147, f32[12,512,1024]{2,1,0:T(8,128)} %get-tuple-element.79, f32[12,512]{1,0:T(8,128)S(1)} %log_add_fusion, pred[512,1024]{1,0:T(8,128)(4,1)S(1)} %get-tuple-element.75), kind=kOutput, calls=%fused_computation.77 | convolution fusion | flops 830865408 | bytes 28073984 | tf_op jit(solution)/shard_map/hqk,khd->qhd/dot_general | solution.py:306
  170.4 12.6 %convolution_convert_fusion.9 = bf16[12,64,512]{2,1,0:T(8,128)(2,1)} fusion(bf16[1024,12,64]{0,2,1:T(8,128)(2,1)S(1)} %bitcast.149, f32[12,512,1024]{2,1,0:T(8,128)} %get-tuple-element.81, f32[12,512]{1,0:T(8,128)S(1)} %log_add_fusion.1, pred[512,1024]{1,0:T(8,128)(4,1)S(1)} %get-tuple-element.74), kind=kOutput, calls=%fused_computation.78 | convolution fusion | flops 830865408 | bytes 28073984 | tf_op jit(solution)/shard_map/hqk,khd->qhd/dot_general | solution.py:306
  189.0 12.5 %multiply_convert_fusion.2 = (bf16[1024,3072]{1,0:T(8,128)(2,1)}, f32[1024,3072]{1,0:T(8,128)}) fusion(f32[3072]{0:T(1024)S(1)} %add.170, bf16[768,3072]{1,0:T(8,128)(2,1)} %all-gather.6.cloned.1.call-done, f32[1024,768]{1,0:T(8,128)} %copy-done.7, f32[768]{0:T(1024)S(1)} %copy-done.44, f32[768]{0:T(1024)S(1)} %copy-done.37, f32[1024]{0:T(1024)S(1)} %add_rsqrt_fusion.1, ...), kind=kOutput, calls=%fused_computation.21 | convolution fusion | flops 4854644736 | bytes 26765312 | tf_op jit(solution)/shard_map/dot_general | solution.py:271
  201.6 9.3 %fusion.53 = (f32[1024]{0:T(1024)S(1)}, f32[1024,768]{1,0:T(8,128)S(1)}) fusion(f32[768]{0:T(1024)S(1)} %copy-done.45, bf16[1024,3072]{1,0:T(8,128)(2,1)} %get-tuple-element.84, bf16[3072,768]{1,0:T(8,128)(2,1)} %all-gather.8.cloned.1.call-done, f32[768]{0:T(1024)S(1)} %copy-done.44, f32[768]{0:T(1024)S(1)} %copy-done.37, f32[1024]{0:T(1024)S(1)} %add_rsqrt_fusion.1, ...), kind=kOutput, calls=%fused_computation.139 | convolution fusion | flops 4837342208 | bytes 17323008 | tf_op jit(solution)/shard_map/dot_general | solution.py:271
  216.7 7.1 %convolution_convert_fusion.1 = bf16[3072,768]{1,0:T(8,128)(2,1)} fusion(bf16[1024,3072]{1,0:T(8,128)(2,1)S(1)} %bitcast.206, f32[1024,768]{1,0:T(8,128)S(1)} %get-tuple-element.62), kind=kOutput, calls=%fused_computation.25 | convolution fusion | flops 4834983936 | bytes 14155776 | tf_op jit(solution)/shard_map/dot_general | solution.py:279
  223.8 12.5 %fusion.54 = (bf16[3072]{0:T(1024)(128)(2,1)}, bf16[1024,3072]{1,0:T(8,128)(2,1)S(1)}) fusion(f32[1024,3072]{1,0:T(8,128)} %get-tuple-element.85, f32[3072]{0:T(1024)S(1)} %add.170, bf16[3072,768]{1,0:T(8,128)(2,1)S(1)} %bitcast.194, f32[1024,768]{1,0:T(8,128)S(1)} %get-tuple-element.62), kind=kOutput, calls=%fused_computation.140 | convolution fusion | flops 4876661760 | bytes 26757120 | tf_op jit(solution)/shard_map/dot_general | solution.py:275
  236.3 8.1 %convolution_convert_fusion = bf16[768,3072]{1,0:T(8,128)(2,1)} fusion(bf16[1024,3072]{1,0:T(8,128)(2,1)S(1)} %get-tuple-element.102, f32[1024,768]{1,0:T(8,128)S(1)} %copy-done.8, f32[768]{0:T(1024)S(1)} %copy-done.44, f32[768]{0:T(1024)S(1)} %copy-done.37, f32[1024]{0:T(1024)S(1)} %add_rsqrt_fusion.1, f32[1024]{0:T(1024)S(1)} %broadcast_multiply_fusion.4), kind=kOutput, calls=%fused_computation.24 | convolution fusion | flops 4838129664 | bytes 14170112 | tf_op jit(solution)/shard_map/dot_general | solution.py:279
  244.4 6.1 %multiply_reduce_fusion.2 = (bf16[768]{0:T(1024)(128)(2,1)S(1)}, f32[1024]{0:T(1024)S(1)}, f32[1024]{0:T(1024)S(1)}, bf16[768]{0:T(1024)(128)(2,1)S(1)}, f32[1024,768]{1,0:T(8,128)S(1)}) fusion(f32[1024,768]{1,0:T(8,128)S(1)} %copy-done.8, f32[1024]{0:T(1024)S(1)} %add_rsqrt_fusion.1, f32[1024]{0:T(1024)S(1)} %broadcast_multiply_fusion.4, ...), kind=kOutput, calls=%fused_computation.45 | convolution fusion | flops 4839698432 | bytes 20469760 | tf_op jit(solution)/shard_map/dot_general | solution.py:275
  256.8 13.3 %bitcast_reduce_fusion.1 = (bf16[12,64]{1,0:T(8,128)(2,1)S(1)}, bf16[12,64,1024]{2,1,0:T(8,128)(2,1)}) fusion(bf16[512,12,64]{0,2,1:T(8,128)(2,1)S(1)} %bitcast.164, f32[12,512,1024]{2,1,0:T(8,128)} %get-tuple-element.81, f32[12,512]{1,0:T(8,128)S(1)} %log_add_fusion.1, pred[512,1024]{1,0:T(8,128)(4,1)S(1)} %get-tuple-element.74), kind=kOutput, calls=%fused_computation.71 | convolution fusion | flops 832044288 | bytes 28075520 | tf_op jit(solution)/shard_map/hqk,qhd->khd/dot_general | solution.py:318
  270.1 21.3 %multiply_reduce_fusion.1 = (f32[12,512]{1,0:T(8,128)S(1)}, f32[12,512,1024]{2,1,0:T(8,128)}) fusion(f32[12,512,1024]{2,1,0:T(8,128)} %get-tuple-element.81, f32[12,512]{1,0:T(8,128)S(1)} %log_add_fusion.1, pred[512,1024]{1,0:T(8,128)(4,1)S(1)} %get-tuple-element.74, bf16[512,12,64]{0,2,1:T(8,128)(2,1)S(1)} %bitcast.165, bf16[1024,12,64]{0,2,1:T(8,128)(2,1)S(1)} %bitcast.150), kind=kOutput, calls=%fused_computation.3 | convolution fusion | flops 836757504 | bytes 53264384 | tf_op jit(solution)/shard_map/qhd,khd->hqk/dot_general | solution.py:313
  291.4 17.2 %multiply_convert_fusion.1 = bf16[12,512,1024]{2,1,0:T(8,128)(2,1)S(1)} fusion(f32[12,512,1024]{2,1,0:T(8,128)} %get-tuple-element.92, f32[12,512,1024]{2,1,0:T(8,128)} %get-tuple-element.81, f32[12,512]{1,0:T(8,128)S(1)} %get-tuple-element.91, f32[12,512]{1,0:T(8,128)S(1)} %log_add_fusion.1, pred[512,1024]{1,0:T(8,128)(4,1)} %copy-done.6), kind=kLoop, calls=%fused_computation.2 | loop fusion | flops 37748736 | bytes 63488000 | tf_op jit(solution)/shard_map/convert_element_type | solution.py:315
  308.6 6.2 %bitcast_reduce_fusion.3 = (bf16[12,64]{1,0:T(8,128)(2,1)S(1)}, bf16[12,64,512]{2,1,0:T(8,128)(2,1)}) fusion(bf16[1024,12,64]{0,2,1:T(8,128)(2,1)} %bitcast.140, bf16[12,512,1024]{2,1,0:T(8,128)(2,1)S(1)} %multiply_convert_fusion.1), kind=kOutput, calls=%fused_computation.82 | convolution fusion | flops 806485248 | bytes 14943744 | tf_op jit(solution)/shard_map/hqk,khd->qhd/dot_general | solution.py:316
  319.6 13.1 %bitcast_reduce_fusion = (bf16[12,64]{1,0:T(8,128)(2,1)S(1)}, bf16[12,64,1024]{2,1,0:T(8,128)(2,1)}) fusion(bf16[512,12,64]{0,2,1:T(8,128)(2,1)S(1)} %bitcast.162, f32[12,512,1024]{2,1,0:T(8,128)} %get-tuple-element.79, f32[12,512]{1,0:T(8,128)S(1)} %log_add_fusion, pred[512,1024]{1,0:T(8,128)(4,1)S(1)} %copy-done.4), kind=kOutput, calls=%fused_computation.70 | convolution fusion | flops 832044288 | bytes 28075520 | tf_op jit(solution)/shard_map/hqk,qhd->khd/dot_general | solution.py:318
  332.7 21.3 %multiply_reduce_fusion = (f32[12,512]{1,0:T(8,128)S(1)}, f32[12,512,1024]{2,1,0:T(8,128)}) fusion(f32[12,512,1024]{2,1,0:T(8,128)} %get-tuple-element.79, f32[12,512]{1,0:T(8,128)S(1)} %log_add_fusion, pred[512,1024]{1,0:T(8,128)(4,1)S(1)} %copy-done.5, bf16[512,12,64]{0,2,1:T(8,128)(2,1)S(1)} %bitcast.163, bf16[1024,12,64]{0,2,1:T(8,128)(2,1)S(1)} %bitcast.148), kind=kOutput, calls=%fused_computation.1 | convolution fusion | flops 836757504 | bytes 53264384 | tf_op jit(solution)/shard_map/qhd,khd->hqk/dot_general | solution.py:313
  354.0 17.2 %multiply_convert_fusion = bf16[12,512,1024]{2,1,0:T(8,128)(2,1)S(1)} fusion(f32[12,512,1024]{2,1,0:T(8,128)} %get-tuple-element.90, f32[12,512,1024]{2,1,0:T(8,128)} %get-tuple-element.79, f32[12,512]{1,0:T(8,128)S(1)} %get-tuple-element.89, f32[12,512]{1,0:T(8,128)S(1)} %log_add_fusion, pred[512,1024]{1,0:T(8,128)(4,1)} %copy-done.3), kind=kLoop, calls=%fused_computation | loop fusion | flops 37748736 | bytes 63488000 | tf_op jit(solution)/shard_map/convert_element_type | solution.py:315
  371.2 6.2 %bitcast_reduce_fusion.2 = (bf16[12,64]{1,0:T(8,128)(2,1)S(1)}, bf16[12,64,512]{2,1,0:T(8,128)(2,1)}) fusion(bf16[1024,12,64]{0,2,1:T(8,128)(2,1)} %bitcast.138, bf16[12,512,1024]{2,1,0:T(8,128)(2,1)S(1)} %multiply_convert_fusion), kind=kOutput, calls=%fused_computation.81 | convolution fusion | flops 806485248 | bytes 14943744 | tf_op jit(solution)/shard_map/hqk,khd->qhd/dot_general | solution.py:316
  407.9 6.2 %bitcast_convert_fusion = bf16[768,768]{1,0:T(8,128)(2,1)} fusion(bf16[1,1024,768]{2,1,0:T(8,128)(2,1)S(1)} %copy-done.18, bf16[1,1024,768]{2,1,0:T(8,128)(2,1)} %copy.86, bf16[2,512,768]{1,2,0:T(8,128)(2,1)} %collective-permute-done, bf16[2,512,768]{1,2,0:T(8,128)(2,1)} %bitcast.1), kind=kOutput, calls=%fused_computation.61 | convolution fusion | flops 2424373248 | bytes 7471104 | tf_op jit(solution)/shard_map/dot_general | solution.py:279
  414.1 5.5 %bitcast_convert_fusion.1 = bf16[768,768]{1,0:T(8,128)(2,1)} fusion(bf16[1,1024,768]{2,1,0:T(8,128)(2,1)S(1)} %copy-done.19, bf16[1,1024,768]{2,1,0:T(8,128)(2,1)S(1)} %copy-done.17, bf16[2,512,768]{1,2,0:T(8,128)(2,1)} %collective-permute-done, bf16[2,512,768]{1,2,0:T(8,128)(2,1)} %bitcast.1), kind=kOutput, calls=%fused_computation.62 | convolution fusion | flops 2424373248 | bytes 7471104 | tf_op jit(solution)/shard_map/dot_general | solution.py:279
  419.6 103.4 %ring_scatter.1 = (f32[96,768]{1,0:T(8,128)}, f32[24,3072]{1,0:T(8,128)}, f32[24,768]{1,0:T(8,128)}, f32[24,768]{1,0:T(8,128)}, f32[24,768]{1,0:T(8,128)}, /*index=5*/f32[24,768]{1,0:T(8,128)}, f32[24,128]{1,0:T(8,128)}) custom-call(bf16[32,96,768]{2,1,0:T(8,128)(2,1)} %bitcast.151, bf16[32,24,3072]{2,1,0:T(8,128)(2,1)} %bitcast.152, ...), custom_call_target="tpu_custom_call" | custom-call | tf_op jit(solution)/shard_map/ring_scatter/pallas_call | solution.py:147
  (255 shorter events, 105.2 us)
Async XLA Ops:
  7.3 76.9 %copy-start.48 = (s32[1,2]{1,0:T(1,128)S(1)}, s32[1,2]{1,0:T(1,128)}, u32[]{:S(2)}) copy-start(s32[1,2]{1,0:T(1,128)} %param.34) | copy-start | bytes 28
  7.3 78.8 %copy-start = (bf16[1,2,512,768]{3,2,1,0:T(8,128)(2,1)S(1)}, bf16[1,2,512,768]{3,2,1,0:T(8,128)(2,1)}, u32[]{:S(2)}) copy-start(bf16[1,2,512,768]{3,2,1,0:T(8,128)(2,1)} %param.35) | copy-start | bytes 4718596
  7.3 175.7 %all-gather.4.cloned.1.call-start = ((), (), s32[]{:S(2)}) async-start(), calls=%async_computation | async-start | bytes 1216512 | tf_op jit(solution)/shard_map/all_gather | solution.py:375
  8.0 180.9 %all-gather.6.cloned.1.call-start = ((), (), s32[]{:S(2)}) async-start(), calls=%async_computation.1 | async-start | bytes 4866048 | tf_op jit(solution)/shard_map/all_gather | solution.py:375
  8.8 192.8 %all-gather.8.cloned.1.call-start = ((), (), s32[]{:S(2)}) async-start(), calls=%async_computation.2 | async-start | bytes 4866048 | tf_op jit(solution)/shard_map/all_gather | solution.py:375
  11.5 77.7 %copy-start.26 = (bf16[1,2,512,768]{3,2,1,0:T(8,128)(2,1)S(1)}, bf16[1,2,512,768]{3,2,1,0:T(8,128)(2,1)}, u32[]{:S(2)}) copy-start(bf16[1,2,512,768]{3,2,1,0:T(8,128)(2,1)} %param.18) | copy-start | bytes 4718596
  11.5 82.2 %collective-permute-start = (bf16[2,512,768]{1,2,0:T(8,128)(2,1)}, bf16[2,512,768]{1,2,0:T(8,128)(2,1)}, u32[]{:S(2)}, u32[]{:S(2)}) collective-permute-start(bf16[2,512,768]{1,2,0:T(8,128)(2,1)} %bitcast.1), channel_id=1, source_target_pairs={{0,16},{1,17},{2,18},{3,19},{4,20},{5,21},{6,22},{7,23},{8,24},{9,... | collective-permute-start | bytes 4718600 | tf_op jit(solution)/shard_map/ppermute | solution.py:358
  92.9 15.1 %copy-start.9 = (bf16[512,768]{0,1:T(8,128)(2,1)}, bf16[512,768]{0,1:T(8,128)(2,1)S(1)}, u32[]{:S(2)}) copy-start(bf16[512,768]{0,1:T(8,128)(2,1)S(1)} %get-tuple-element.73) | copy-start | bytes 2359300
  93.6 64.4 %copy-start.3 = (pred[512,1024]{1,0:T(8,128)(4,1)}, pred[512,1024]{1,0:T(8,128)(4,1)S(1)}, u32[]{:S(2)}) copy-start(pred[512,1024]{1,0:T(8,128)(4,1)S(1)} %get-tuple-element.75) | copy-start | bytes 1572868
  93.6 176.5 %copy-start.6 = (pred[512,1024]{1,0:T(8,128)(4,1)}, pred[512,1024]{1,0:T(8,128)(4,1)S(1)}, u32[]{:S(2)}) copy-start(pred[512,1024]{1,0:T(8,128)(4,1)S(1)} %get-tuple-element.74) | copy-start | bytes 1572868
  108.0 23.2 %copy-start.2 = (bf16[1024,768]{0,1:T(8,128)(2,1)}, bf16[1024,768]{0,1:T(8,128)(2,1)S(1)}, u32[]{:S(2)}) copy-start(bf16[1024,768]{0,1:T(8,128)(2,1)S(1)} %get-tuple-element.66) | copy-start | bytes 4718596
  170.4 12.7 %copy-start.62 = (bf16[12,64,512]{2,1,0:T(8,128)(2,1)}, bf16[12,64,512]{2,1,0:T(8,128)(2,1)S(1)}, u32[]{:S(2)}) copy-start(bf16[12,64,512]{2,1,0:T(8,128)(2,1)S(1)} %convolution_convert_fusion.8) | copy-start | bytes 2359300
  170.4 12.7 %copy-start.46 = (f32[768]{0:T(1024)S(1)}, f32[768]{0:T(1024)}, u32[]{:S(2)}) copy-start(f32[768]{0:T(1024)} %get-tuple-element.50) | copy-start | bytes 9220
  189.0 12.5 %copy-start.45 = (f32[768]{0:T(1024)S(1)}, f32[768]{0:T(1024)}, u32[]{:S(2)}) copy-start(f32[768]{0:T(1024)} %get-tuple-element.47) | copy-start | bytes 9220
  216.7 27.8 %slice-start.2 = ((s8[4718592]{0:T(1024)(128)(4,1)}), s8[4194304]{0:T(1024)(128)(4,1)S(1)}, s32[]{:S(2)}) async-start(s8[4718592]{0:T(1024)(128)(4,1)} %bitcast.191), calls=%async_computation.5 | async-start | bytes 8388608
  223.8 12.5 %copy-start.8 = (f32[1024,768]{1,0:T(8,128)S(1)}, f32[1024,768]{1,0:T(8,128)}, u32[]{:S(2)}) copy-start(f32[1024,768]{1,0:T(8,128)} %copy-done.7) | copy-start | bytes 9437188
  223.8 20.6 %slice-start.3 = ((s8[4718592]{0:T(1024)(128)(4,1)}), s8[524288]{0:T(1024)(128)(4,1)S(1)}, s32[]{:S(2)}) async-start(s8[4718592]{0:T(1024)(128)(4,1)} %bitcast.191), calls=%async_computation.6 | async-start | bytes 1048576
  256.8 13.3 %copy-start.16 = (bf16[1024,768]{0,1:T(8,128)(2,1)S(1)}, bf16[1024,768]{0,1:T(8,128)(2,1)}, u32[]{:S(2)}) copy-start(bf16[1024,768]{0,1:T(8,128)(2,1)} %copy-done.15) | copy-start | bytes 4718596
  319.6 13.1 %copy-start.5 = (pred[512,1024]{1,0:T(8,128)(4,1)S(1)}, pred[512,1024]{1,0:T(8,128)(4,1)}, u32[]{:S(2)}) copy-start(pred[512,1024]{1,0:T(8,128)(4,1)} %copy-done.3) | copy-start | bytes 1572868
  319.6 13.1 %copy-start.14 = (bf16[1024,768]{0,1:T(8,128)(2,1)S(1)}, bf16[1024,768]{0,1:T(8,128)(2,1)}, u32[]{:S(2)}) copy-start(bf16[1024,768]{0,1:T(8,128)(2,1)} %copy-done.13) | copy-start | bytes 4718596
  319.6 13.1 %copy-start.25 = (bf16[512,768]{0,1:T(8,128)(2,1)S(1)}, bf16[512,768]{0,1:T(8,128)(2,1)}, u32[]{:S(2)}) copy-start(bf16[512,768]{0,1:T(8,128)(2,1)} %get-tuple-element.71) | copy-start | bytes 2359300
  400.8 129.6 %collective-permute-start.1 = (bf16[2,512,768]{2,1,0:T(8,128)(2,1)}, bf16[2,512,768]{2,1,0:T(8,128)(2,1)}, u32[]{:S(2)}, u32[]{:S(2)}) collective-permute-start(bf16[2,512,768]{2,1,0:T(8,128)(2,1)} %slice.191), channel_id=1, source_target_pairs={{16,0},{17,1},{18,2},{19,3},{20,4},{21,5},{22,6},{23,7},{24,8},{25... | collective-permute-start | bytes 4718600 | tf_op jit(solution)/shard_map/ppermute | solution.py:454
  419.6 106.6 %copy-start.29 = (bf16[12,64,512]{2,1,0:T(8,128)(2,1)S(1)}, bf16[12,64,512]{2,1,0:T(8,128)(2,1)}, u32[]{:S(2)}) copy-start(bf16[12,64,512]{2,1,0:T(8,128)(2,1)} %get-tuple-element.94) | copy-start | bytes 2359300
  419.6 110.8 %slice-start = ((s8[6291456]{0:T(1024)(128)(4,1)}), s8[2097152]{0:T(1024)(128)(4,1)S(1)}, s32[]{:S(2)}) async-start(s8[6291456]{0:T(1024)(128)(4,1)} %bitcast.154), calls=%async_computation.3 | async-start | bytes 4194304
  (54 other events, 314.3 us)
Sparse Core Ops, SparseCore 0:
  11.0 55.2 all-gather.3
  69.2 62.0 all-gather.5
  134.2 61.8 all-gather.7
